TPU v7x, 256 devices: a whole 4x4x8 slice. The times are simulated.
256 devices in a mesh: seq: 4 (over y), lat: 32 (over x_hi, z, core), batch: 2 (over x_lo).
Axes of the slice: x: 4 (x_hi: 2, x_lo: 2; x = x_hi * 2 + x_lo), y: 4, z: 8, core: 2. Of those that a mesh axis runs over, the one named last changes fastest.
Arguments:
- activations: bfloat16 [2, 1024, 3584], P('batch', 'seq'), may hold values from -6 to 6
- dictionary: bfloat16 [32768, 3584], P('lat'), may hold values from -0.09375 to 0.09375
- topk_ids: int32 [2, 1024, 64], P('batch', 'seq'), may hold values from 0 to 32767, as said below
- kernel_taps: float32 [9, 32768], P(None, 'lat'), may hold values from -2 to 2
- enc_bias: float32 [32768], P('lat'), may hold values from -3 to 3
Outputs:
- grad_dictionary: float32 [32768, 3584], P('lat', ('seq', 'batch'))
- grad_taps: float32 [9, 32768], P(None, 'lat')
- grad_bias: float32 [32768], P('lat')
Inputs may be any that keep to these rules, and one draw needn't show every extreme that they name: `topk_ids`: each position names 64 different latents.
All inputs are finite; a program needn't handle non-finite values.
Results may differ from a plain program's by a relative error of at most 0.017.
Values may be sent and summed in bfloat16 or wider, within the bound.
A program may use at most 128 MiB of HBM per device.

v0:
```python
import jax
import jax.numpy as jnp
from jax import lax
from jax.sharding import Mesh
from jax.sharding import PartitionSpec as P

TAPS = 9
HALF = 4
LAT = ("lat_0", "lat_1", "lat_2")


def extended(cells, sides, width):
    for axis, dim in sides:
        count = lax.axis_size(axis)
        ends = count - 1
        head = lax.slice_in_dim(cells, 0, width, axis=dim)
        tail = lax.slice_in_dim(cells, cells.shape[dim] - width, cells.shape[dim], axis=dim)
        cells = jnp.concatenate(
            [
                lax.ppermute(tail, axis, [(i, (i + 1) % count) for i in range(ends)]),
                cells,
                lax.ppermute(head, axis, [((i + 1) % count, i) for i in range(ends)]),
            ],
            axis=dim,
        )
    return cells


def split_up(shard, dim, devices):
    shape = shard.shape
    blocks = shard.reshape(*shape[:dim], devices, shape[dim] // devices, *shape[dim + 1 :])
    return jnp.moveaxis(blocks, dim, 0)


def sum_at_owner(shard, axis, dim):
    devices = lax.axis_size(axis)
    blocks = lax.all_to_all(split_up(shard, dim, devices), axis, 0, 0, tiled=True)
    return jnp.sum(blocks.astype(jnp.float32), axis=0)


def summed_rows(shard, axes, dim):
    far, near = axes
    blocks = split_up(shard, dim, lax.axis_size(far))
    nearer = sum_at_owner(blocks, near, dim + 1)
    arrived = lax.all_to_all(
        nearer.astype(jnp.bfloat16), far, split_axis=0, concat_axis=0, tiled=True
    )
    return arrived.astype(jnp.float32).sum(axis=0)


def rows_for(lines, devices):
    spare = -len(lines) % devices
    return jnp.pad(lines, [(0, spare)] + [(0, 0)] * (lines.ndim - 1))


def copy_for_each(shard, axis):
    devices = lax.axis_size(axis)
    return lax.all_to_all(
        jnp.broadcast_to(shard[None], (devices, *shard.shape)), axis, 0, 0, tiled=True
    )


def laid_out(blocks, dim):
    shape = list(blocks.shape[1:])
    shape[dim] *= blocks.shape[0]
    return jnp.moveaxis(blocks, 0, dim).reshape(shape)


def whole_of(shard, axes, dim):
    far, near = axes
    blocks = copy_for_each(copy_for_each(shard, far), near)
    return laid_out(blocks.swapaxes(0, 1).reshape(-1, *shard.shape), dim)


def sum_by_parts(shard, axes):
    lines = shard.reshape(-1, shard.shape[-1])
    own = summed_rows(rows_for(lines, lax.axis_size(axes[0]) * lax.axis_size(axes[1])), axes, 0)
    whole = whole_of(own.astype(jnp.bfloat16), axes, 0)
    return whole[: len(lines)].reshape(shard.shape).astype(jnp.float32)


def of_everyone(shard, axis):
    everything = copy_for_each(shard, axis)
    return jnp.sum(everything.astype(jnp.float32), axis=0)


def body(activations, dictionary, topk_ids, kernel_taps, enc_bias):
    token_rows = activations[0]
    chosen_ids = topk_ids[0]
    positions = token_rows.shape[0]
    width_local = dictionary.shape[0]
    latent_in = jnp.einsum("td,ld->tl", token_rows, dictionary, preferred_element_type=jnp.float32)
    padded_in = extended(latent_in.astype(jnp.bfloat16), (("seq", 0),), HALF).astype(
        latent_in.dtype
    )
    preact = jnp.zeros(latent_in.shape, jnp.float32)
    for tap_index in range(TAPS):
        preact = (
            preact + kernel_taps[tap_index][None, :] * padded_in[tap_index : tap_index + positions]
        )
    preact = preact + enc_bias[None, :]
    first_latent = lax.axis_index(LAT) * width_local
    latent_ids = first_latent + jnp.arange(width_local, dtype=jnp.int32)
    active = jnp.any(chosen_ids[:, :, None] == latent_ids[None, None, :], axis=1).astype(
        jnp.float32
    )
    latents = (active * preact).astype(jnp.bfloat16)
    recon_part = jnp.einsum("tl,ld->td", latents, dictionary, preferred_element_type=jnp.float32)
    recon_full = sum_by_parts(recon_part.astype(jnp.bfloat16), (("lat_0", "lat_1"), "lat_2"))
    error_rows = (recon_full - token_rows.astype(jnp.float32)).astype(jnp.bfloat16)
    grad_code = jnp.einsum("td,ld->tl", error_rows, dictionary, preferred_element_type=jnp.float32)
    decoder_term = jnp.einsum("tl,td->ld", latents, error_rows, preferred_element_type=jnp.float32)
    grad_pre = active * grad_code
    padded_grad = extended(grad_pre.astype(jnp.bfloat16), (("seq", 0),), HALF).astype(
        grad_pre.dtype
    )
    grad_wide = jnp.zeros(grad_pre.shape, jnp.float32)
    for tap_index in range(TAPS):
        begin = 2 * HALF - tap_index
        grad_wide = (
            grad_wide + kernel_taps[tap_index][None, :] * padded_grad[begin : begin + positions]
        )
    grad_in = grad_wide.astype(jnp.bfloat16)
    tap_parts = jnp.stack(
        [
            jnp.sum(grad_pre * padded_in[tap_index : tap_index + positions], axis=0)
            for tap_index in range(TAPS)
        ]
    )
    bias_part = jnp.sum(grad_pre, axis=0)
    grad_taps, grad_bias = (
        of_everyone(tap_parts.astype(jnp.bfloat16), ("seq", "batch")).astype(jnp.float32),
        of_everyone(bias_part.astype(jnp.bfloat16), ("seq", "batch")).astype(jnp.float32),
    )
    dict_term = decoder_term + jnp.einsum(
        "tl,td->ld", grad_in, token_rows, preferred_element_type=jnp.float32
    )
    dict_rounded = lax.optimization_barrier(dict_term.astype(jnp.bfloat16)).astype(jnp.float32)
    grad_dictionary = lax.psum_scatter(
        dict_rounded.astype(jnp.bfloat16), ("seq", "batch"), scatter_dimension=1, tiled=True
    ).astype(jnp.float32)
    return (grad_dictionary, grad_taps, grad_bias)


def solution(mesh):
    finer = Mesh(
        mesh.devices.reshape(mesh.shape["seq"], 2, 8, 2, mesh.shape["batch"]),
        ("seq", "lat_0", "lat_1", "lat_2", "batch"),
    )
    return jax.shard_map(
        body,
        mesh=finer,
        in_specs=(
            P("batch", "seq", None),
            P(LAT, None),
            P("batch", "seq", None),
            P(None, LAT),
            P(LAT),
        ),
        out_specs=(P(LAT, ("seq", "batch")), P(None, LAT), P(LAT)),
        check_vma=False,
    )
```

profile of v0, /device:TPU:32, one launch (start us, length us, event | category | flops | bytes accessed | tf_op | source)
XLA Modules:
  0.0 316.1 jit_solution(15059492138934945247)
XLA Ops:
  7.2 5.7 %fusion.4 = bf16[256,1024]{1,0:T(8,128)(2,1)S(1)} fusion(bf16[1024,3584]{1,0:T(8,128)(2,1)} %param.6, bf16[1,256,3584]{2,1,0:T(8,128)(2,1)} %param.5), kind=kOutput, calls=%fused_computation.11 | convolution fusion | flops 1879310336 | bytes 9699328 | tf_op jit(solution)/shard_map/td,ld->tl/dot_general | solution.py:92
  13.0 1.3 collective-permute-start.1
  14.3 4.5 %collective-permute-start = (bf16[4,1024]{1,0:T(4,128)(2,1)S(1)}, bf16[4,1024]{1,0:T(4,128)(2,1)S(1)}, u32[]{:S(2)}, u32[]{:S(2)}) collective-permute-start(bf16[4,1024]{1,0:T(4,128)(2,1)S(1)} %get-tuple-element.34), channel_id=1, source_target_pairs={{0,64},{64,128},{128,192},{1,65},{65,129},{129,193},{2,66},{66,130... | collective-permute-start | bytes 24584 | tf_op jit(solution)/shard_map/ppermute | solution.py:20
  19.0 9.4 %compare_reduce_fusion = pred[256,1024]{1,0:T(8,128)(4,1)S(1)} fusion(s32[1024]{0:T(1024)S(1)} %iota_add_fusion, s32[256,64]{1,0:T(8,128)S(1)} %copy.27), kind=kLoop, calls=%fused_computation | loop fusion | flops 33292288 | bytes 331776 | tf_op jit(solution)/shard_map/reduce_or | solution.py:104
  29.1 1.3 select_convert_fusion
  30.5 1.7 copy-done.6
  32.2 2.1 convolution_convert_fusion
  34.4 5.2 %all_to_all.31 = bf16[2,16,8,3584]{3,2,1,0:T(8,128)(2,1)S(1)} all-to-all(bf16[2,16,8,3584]{3,2,1,0:T(8,128)(2,1)S(1)} %bitcast.38), channel_id=1, replica_groups=mesh['seq'=4,'lat_0'=2,'lat_1'=8,'lat_2'=2,'batch'=2] {'lat_2'}, dimensions={0} | all-to-all | bytes 3670016 | tf_op jit(solution)/shard_map/all_to_all | solution.py:37
  39.6 1.5 reduce_sum.132
  41.1 36.7 %all_to_all.32 = bf16[16,8,3584]{2,1,0:T(8,128)(2,1)S(1)} all-to-all(bf16[16,8,3584]{2,1,0:T(8,128)(2,1)} %reduce_sum.132), channel_id=1, replica_groups=mesh['seq'=4,'lat_0'=2,'lat_1'=8,'lat_2'=2,'batch'=2] {'lat_0','lat_1'}, dimensions={0} | all-to-all | bytes 1835008 | tf_op jit(solution)/shard_map/all_to_all | solution.py:45
  78.0 30.0 %all_to_all.33 = bf16[16,8,3584]{2,1,0:T(8,128)(2,1)S(1)} all-to-all(bf16[16,8,3584]{2,1,0:T(8,128)(2,1)S(1)} %broadcast_in_dim.8), channel_id=1, replica_groups=mesh['seq'=4,'lat_0'=2,'lat_1'=8,'lat_2'=2,'batch'=2] {'lat_0','lat_1'}, dimensions={0} | all-to-all | bytes 1835008 | tf_op jit(solution)/shard_map/all_to_all | solution.py:58
  108.1 5.2 %all_to_all.34 = bf16[2,16,8,3584]{3,2,1,0:T(8,128)(2,1)S(1)} all-to-all(bf16[2,16,8,3584]{3,2,1,0:T(8,128)(2,1)S(1)} %broadcast_in_dim.9), channel_id=1, replica_groups=mesh['seq'=4,'lat_0'=2,'lat_1'=8,'lat_2'=2,'batch'=2] {'lat_2'}, dimensions={0} | all-to-all | bytes 3670016 | tf_op jit(solution)/shard_map/all_to_all | solution.py:58
  113.8 1.1 copy-done
  115.3 0.5 copy-done.2
  115.8 6.3 %multiply_reduce_fusion = (bf16[1024]{0:T(1024)(128)(2,1)S(1)}, bf16[1024]{0:T(1024)(128)(2,1)S(1)}, bf16[1024]{0:T(1024)(128)(2,1)S(1)}, bf16[1024]{0:T(1024)(1...) fusion(f32[264,1024]{1,0:T(8,128)S(1)} %maximum_convert_fusion,, ...), kind=kOutput, calls=%fused_computation.30 | convolution fusion | flops 1884542976 | bytes 19419136 | tf_op jit(solution)/shard_map/td,ld->tl/dot_general | solution.py:111
  122.1 1.3 collective-permute-start.3
  123.4 4.7 %collective-permute-start.2 = (bf16[4,1024]{1,0:T(4,128)(2,1)S(1)}, bf16[4,1024]{1,0:T(4,128)(2,1)S(1)}, u32[]{:S(2)}, u32[]{:S(2)}) collective-permute-start(bf16[4,1024]{1,0:T(4,128)(2,1)S(1)} %get-tuple-element.32), channel_id=1, source_target_pairs={{0,64},{64,128},{128,192},{1,65},{65,129},{129,193},{2,66},{66,130... | collective-permute-start | bytes 24584 | tf_op jit(solution)/shard_map/ppermute | solution.py:20
  128.1 7.3 %fusion.29 = f32[1024,3584]{1,0:T(8,128)} fusion(bf16[256,1024]{1,0:T(8,128)(2,1)S(1)} %select_convert_fusion, bf16[256,3584]{1,0:T(8,128)(2,1)S(1)} %fusion), kind=kOutput, calls=%fused_computation.57 | convolution fusion | flops 1879048192 | bytes 17039360 | tf_op jit(solution)/shard_map/tl,td->ld/dot_general | solution.py:112
  135.6 8.7 %add_convert_fusion = bf16[1024,3584]{1,0:T(8,128)(2,1)} fusion(f32[1024,3584]{1,0:T(8,128)} %fusion.29, bf16[1,256,3584]{2,1,0:T(8,128)(2,1)S(1)} %copy-done, f32[264,1024]{1,0:T(8,128)S(1)} %maximum_convert_fusion.1, f32[1024]{0:T(1024)S(1)} %bitcast.57, f32[1024]{0:T(1024)S(1)} %bitcast.59, f32[1024]{0:T(1024)S(1)} %bitcast.45, f32[1024]{0:T(1024)S(1)} %bitcast.47, ...), kind=kOutput, calls=%fused_computation.1 | convolution fusion | flops 1891106816 | bytes 33329152 | tf_op jit(solution)/shard_map/tl,td->ld/dot_general | solution.py:135
  144.3 10.4 %copy.33 = bf16[1024,3584]{0,1:T(8,128)(2,1)} copy(bf16[1024,3584]{1,0:T(8,128)(2,1)} %add_convert_fusion) | data formatting | bytes 14680064
  155.3 0.7 reduce.3
  156.0 0.6 reshape.111
  156.6 4.5 %all-to-all-start.5 = ((bf16[8,2,512]{2,1,0:T(2,128)(2,1)}), bf16[8,2,512]{2,1,0:T(2,128)(2,1)S(1)}, u32[]{:S(2)}, u32[]{:S(2)}) async-start(bf16[8,2,512]{2,1,0:T(2,128)(2,1)} %reshape.111), calls=%async_computation.5 | async-start | bytes 32768 | tf_op jit(solution)/shard_map/all_to_all | solution.py:58
  161.3 6.0 %all-to-all-done.5 = bf16[8,2,512]{2,1,0:T(2,128)(2,1)S(1)} async-done(((bf16[8,2,512]{2,1,0:T(2,128)(2,1)}), bf16[8,2,512]{2,1,0:T(2,128)(2,1)S(1)}, u32[]{:S(2)}, u32[]{:S(2)}) %all-to-all-start.5) | async-done | bytes 16416 | tf_op jit(solution)/shard_map/all_to_all | solution.py:58
  167.4 0.7 broadcast_in_dim.10
  168.1 3.4 %all-to-all-start.4 = ((bf16[8,9,1024]{2,1,0:T(8,128)(2,1)}), bf16[8,9,1024]{2,1,0:T(8,128)(2,1)S(1)}, u32[]{:S(2)}, u32[]{:S(2)}) async-start(bf16[8,9,1024]{2,1,0:T(8,128)(2,1)} %broadcast_in_dim.10), calls=%async_computation.4 | async-start | bytes 524288 | tf_op jit(solution)/shard_map/all_to_all | solution.py:58
  171.5 0.6 convert_reduce_fusion.1
  172.2 9.9 %all-to-all-done.4 = bf16[8,9,1024]{2,1,0:T(8,128)(2,1)S(1)} async-done(((bf16[8,9,1024]{2,1,0:T(8,128)(2,1)}), bf16[8,9,1024]{2,1,0:T(8,128)(2,1)S(1)}, u32[]{:S(2)}, u32[]{:S(2)}) %all-to-all-start.4) | async-done | bytes 147488 | tf_op jit(solution)/shard_map/all_to_all | solution.py:58
  182.0 0.8 convert_reduce_fusion
  182.8 123.4 %reduce-scatter.4.cloned.1.call-done = bf16[448,1024]{1,0:T(8,128)(2,1)} async-done(((bf16[3584,1024]{1,0:T(8,128)(2,1)}), bf16[448,1024]{1,0:T(8,128)(2,1)}) %reduce-scatter.4.cloned.1.call-update) | async-done | bytes 917520
  306.3 1.5 copy.34
  307.7 1.5 copy.32
  (43 shorter events, 2.9 us)
Async XLA Ops:
  7.2 11.7 %copy-start.3 = (s32[1,256,64]{1,2,0:T(8,128)S(1)}, s32[1,256,64]{1,2,0:T(8,128)}, u32[]{:S(2)}) copy-start(s32[1,256,64]{1,2,0:T(8,128)} %param.7) | copy-start | bytes 196612
  7.2 21.2 %copy-start.4 = (f32[9,1024]{1,0:T(8,128)S(1)}, f32[9,1024]{1,0:T(8,128)}, u32[]{:S(2)}) copy-start(f32[9,1024]{1,0:T(8,128)} %param.8) | copy-start | bytes 110596
  7.2 299.1 %reduce-scatter.4.cloned.1.call-start = ((), (), s32[]{:S(2)}) async-start(), calls=%async_computation.7 | async-start | bytes 8257536
  13.0 16.2 %copy-start.5 = (f32[1024]{0:T(1024)S(1)}, f32[1024]{0:T(1024)}, u32[]{:S(2)}) copy-start(f32[1024]{0:T(1024)} %param.9) | copy-start | bytes 12292
  13.0 15.5 %collective-permute-start.1 = (bf16[4,1024]{1,0:T(4,128)(2,1)S(1)}, bf16[4,1024]{1,0:T(4,128)(2,1)S(1)}, u32[]{:S(2)}, u32[]{:S(2)}) collective-permute-start(bf16[4,1024]{1,0:T(4,128)(2,1)S(1)} %get-tuple-element.35), channel_id=1, source_target_pairs={{64,0},{128,64},{192,128},{65,1},{129,65},{193,129},{66,2},{130,66... | collective-permute-start | bytes 24584 | tf_op jit(solution)/shard_map/ppermute | solution.py:22
  14.3 14.2 %collective-permute-start = (bf16[4,1024]{1,0:T(4,128)(2,1)S(1)}, bf16[4,1024]{1,0:T(4,128)(2,1)S(1)}, u32[]{:S(2)}, u32[]{:S(2)}) collective-permute-start(bf16[4,1024]{1,0:T(4,128)(2,1)S(1)} %get-tuple-element.34), channel_id=1, source_target_pairs={{0,64},{64,128},{128,192},{1,65},{65,129},{129,193},{2,66},{66,130... | collective-permute-start | bytes 24584 | tf_op jit(solution)/shard_map/ppermute | solution.py:20
  28.4 0.7 copy-start.1
  29.1 3.1 copy-start.6
  113.3 1.5 copy-start
  114.8 0.9 copy-start.2
  122.1 13.4 %collective-permute-start.3 = (bf16[4,1024]{1,0:T(4,128)(2,1)S(1)}, bf16[4,1024]{1,0:T(4,128)(2,1)S(1)}, u32[]{:S(2)}, u32[]{:S(2)}) collective-permute-start(bf16[4,1024]{1,0:T(4,128)(2,1)S(1)} %get-tuple-element.33), channel_id=1, source_target_pairs={{64,0},{128,64},{192,128},{65,1},{129,65},{193,129},{66,2},{130,66... | collective-permute-start | bytes 24584 | tf_op jit(solution)/shard_map/ppermute | solution.py:22
  123.4 12.1 %collective-permute-start.2 = (bf16[4,1024]{1,0:T(4,128)(2,1)S(1)}, bf16[4,1024]{1,0:T(4,128)(2,1)S(1)}, u32[]{:S(2)}, u32[]{:S(2)}) collective-permute-start(bf16[4,1024]{1,0:T(4,128)(2,1)S(1)} %get-tuple-element.32), channel_id=1, source_target_pairs={{0,64},{64,128},{128,192},{1,65},{65,129},{129,193},{2,66},{66,130... | collective-permute-start | bytes 24584 | tf_op jit(solution)/shard_map/ppermute | solution.py:20
  156.6 10.7 %all-to-all-start.5 = ((bf16[8,2,512]{2,1,0:T(2,128)(2,1)}), bf16[8,2,512]{2,1,0:T(2,128)(2,1)S(1)}, u32[]{:S(2)}, u32[]{:S(2)}) async-start(bf16[8,2,512]{2,1,0:T(2,128)(2,1)} %reshape.111), calls=%async_computation.5 | async-start | bytes 32768 | tf_op jit(solution)/shard_map/all_to_all | solution.py:58
  168.1 13.9 %all-to-all-start.4 = ((bf16[8,9,1024]{2,1,0:T(8,128)(2,1)}), bf16[8,9,1024]{2,1,0:T(8,128)(2,1)S(1)}, u32[]{:S(2)}, u32[]{:S(2)}) async-start(bf16[8,9,1024]{2,1,0:T(8,128)(2,1)} %broadcast_in_dim.10), calls=%async_computation.4 | async-start | bytes 524288 | tf_op jit(solution)/shard_map/all_to_all | solution.py:58
Sparse Core Ops, SparseCore 0:
  154.9 151.3 reduce-scatter.3
where the time goes:
time: 318 us; the launch traced here: 316 us
  waiting for transfers between devices  139 us (44%)
  blocking collectives  77.1 us (24%)
  matrix products  30.1 us (9%)
  starting transfers between devices  19.8 us (6%)
  local copies, waits for them, and re-layouts  19.7 us (6%)
  other arithmetic  15.7 us (5%)
  between operations  14.4 us (5%)
    unnamed x2, waiting for transfers between devices  123 us
    all_to_all x1, blocking collectives, summed_rows(): lax.all_to_all(nearer.astype(jnp.bfloat16), far, split_axis=0, concat_axi...  36.7 us
    all_to_all x2, blocking collectives, copy_for_each(): lax.all_to_all(jnp.broadcast_to(shard[None], (devices, *shard.shape)), ax...  35.2 us
    unnamed x19, local copies, waits for them, and re-layouts  17.8 us
    all_to_all x2, waiting for transfers between devices, copy_for_each(): lax.all_to_all(jnp.broadcast_to(shard[None], (devices, *shard.shape)), ax...  15.9 us
    reduce_or x1, other arithmetic, body(): jnp.any(chosen_ids[:, :, None] == latent_ids[None, None, :], axis=1)  9.43 us
    ppermute x2, starting transfers between devices, extended(): lax.ppermute(tail, axis, [(i, (i + 1) % count) for i in range(ends)])  9.27 us
    dot_general x1, matrix products, body(): jnp.einsum('tl,td->ld', grad_in, token_rows, preferred_element_type=jnp.f...  8.66 us
  transfers between devices with their start and end apart: 7, of which 3 were waited for; matrix products, arithmetic and copies ran while one was open for 7% of the time, Pallas kernels for 0%

commit v1 on v0

v1 whole, which is shorter than its diff:
```python
import functools

import jax
import jax.numpy as jnp
from jax import lax
from jax.experimental import pallas as pl
from jax.experimental.pallas import tpu as pltpu
from jax.sharding import Mesh
from jax.sharding import PartitionSpec as P

TAPS = 9
HALF = 4
LAT = ("lat_0", "lat_1", "lat_2")
D = 3584
TOK = 256
LATS = 1024
SLOTS = 64
OWN = 448
GROUP = 8
NONE = 64
PIECES = 4
F32 = jnp.float32
BF16 = jnp.bfloat16
MESH = pl.DeviceIdType.MESH
VMEM = pl.BlockSpec(memory_space=pltpu.VMEM)
ANY = pl.BlockSpec(memory_space=pl.ANY)
BIG = 64 * 1024 * 1024 - 65536


def seat():
    return lax.axis_index("seq") * 2 + lax.axis_index("batch")


def peer(delta):
    j = lax.rem(seat() + delta, GROUP)
    return j, {"seq": j // 2, "batch": lax.rem(j, 2)}


def peer_from(delta):
    return lax.rem(seat() + GROUP - delta, GROUP)


def enter(partners):
    barrier = pltpu.get_barrier_semaphore()
    for device in partners:
        pl.semaphore_signal(barrier, inc=1, device_id=device, device_id_type=MESH)
    pl.semaphore_wait(barrier, len(partners))


def group_partners():
    return [peer(delta)[1] for delta in range(1, GROUP)]


def remote(src, dst, send_sem, recv_sem, device):
    return pltpu.make_async_remote_copy(
        src_ref=src,
        dst_ref=dst,
        send_sem=send_sem,
        recv_sem=recv_sem,
        device_id=device,
        device_id_type=MESH,
    )


def opening_kernel(
    act_ref, dict_ref, act8_ref, ids_ref,
    cols_ref, lat_ref, inv_ref, ids8_ref,
    dbuf, dsem, id_send, id_recv, act_send, act_recv, halo_send, halo_recv, own_sem,
):
    me = seat()
    seq = lax.axis_index("seq")
    for c in range(4):
        pltpu.make_async_copy(dict_ref.at[pl.ds(c * 256, 256)], dbuf.at[c], dsem.at[c]).start()
    enter(group_partners())
    sends = []
    for delta in range(1, GROUP):
        _, device = peer(delta)
        copy = remote(
            ids_ref, ids8_ref.at[me], id_send.at[delta - 1], id_recv.at[delta - 1], device
        )
        copy.start()
        sends.append(copy)
    for delta in range(1, GROUP):
        j, device = peer(delta)
        copy = remote(
            act8_ref.at[j], cols_ref.at[me], act_send.at[delta - 1], act_recv.at[delta - 1], device
        )
        copy.start()
        sends.append(copy)
    own_cols = pltpu.make_async_copy(act8_ref.at[me], cols_ref.at[me], own_sem.at[0])
    own_ids = pltpu.make_async_copy(ids_ref, ids8_ref.at[me], own_sem.at[1])
    own_cols.start()
    own_ids.start()

    def encode(c, carry):
        pltpu.make_async_copy(dict_ref.at[pl.ds(0, 256)], dbuf.at[c], dsem.at[c]).wait()
        lanes = pl.ds(pl.multiple_of(c * 256, 256), 256)
        lat_ref[8 : 8 + TOK, lanes] = lax.dot_general(
            act_ref[...], dbuf[c], (((1,), (1,)), ((), ())), preferred_element_type=F32
        )
        return carry

    lax.fori_loop(0, 4, encode, 0)
    left = {"seq": lax.rem(seq + 3, 4)}
    right = {"seq": lax.rem(seq + 1, 4)}
    to_left = remote(
        lat_ref.at[pl.ds(8, 8)], lat_ref.at[pl.ds(8 + TOK, 8)], halo_send.at[0], halo_recv.at[0], left
    )
    to_right = remote(
        lat_ref.at[pl.ds(TOK, 8)], lat_ref.at[pl.ds(0, 8)], halo_send.at[1], halo_recv.at[1], right
    )
    to_left.start()
    to_right.start()
    own_ids.wait()
    for delta in range(1, GROUP):
        pltpu.make_async_copy(ids_ref, ids8_ref.at[0], id_recv.at[delta - 1]).wait()

    first = (
        lax.axis_index("lat_0") * 16 + lax.axis_index("lat_1") * 2 + lax.axis_index("lat_2")
    ) * LATS
    lane = lax.broadcasted_iota(jnp.int32, (16, 128), 1).astype(F32).astype(BF16)

    def slot_rows(block, carry):
        j = block // 8
        row = pl.multiple_of(lax.rem(block, 8) * 16, 16)
        local = ids8_ref[j, pl.ds(row, 16), :] - first
        inside = (local >= 0) & (local < LATS)
        code = jnp.where(inside, local, 8 * 128)
        low = (code & 127).astype(F32).astype(BF16)
        high = (code >> 7).astype(F32).astype(BF16)
        for side in range(2):
            found = [jnp.full((16, 128), NONE, BF16) for _ in range(8)]
            for k in range(SLOTS):
                at = side * SLOTS + k
                here = lane == jnp.broadcast_to(low[:, at : at + 1], (16, 128))
                tile = jnp.where(
                    here, jnp.broadcast_to(high[:, at : at + 1], (16, 128)), jnp.array(8, BF16)
                )
                slot = jnp.array(k, BF16)
                for c in range(8):
                    found[c] = jnp.where(tile == jnp.array(c, BF16), slot, found[c])
            start = pl.multiple_of(j * TOK + side * 128 + row, 16)
            for c in range(8):
                inv_ref[pl.ds(start, 16), c * 128 : (c + 1) * 128] = found[c]
        return carry

    lax.fori_loop(0, 64, slot_rows, 0)

    to_left.wait()
    to_right.wait()
    lat_ref[0:8, :] = jnp.where(seq > 0, lat_ref[0:8, :], 0.0)
    lat_ref[8 + TOK :, :] = jnp.where(seq < 3, lat_ref[8 + TOK :, :], 0.0)
    own_cols.wait()
    for delta in range(1, GROUP):
        pltpu.make_async_copy(act8_ref.at[0], cols_ref.at[0], act_recv.at[delta - 1]).wait()
    for copy in sends:
        copy.wait_send()


def opening(act, dictionary, act8, ids):
    return pl.pallas_call(
        opening_kernel,
        out_shape=(
            jax.ShapeDtypeStruct((GROUP, TOK, OWN), BF16),
            jax.ShapeDtypeStruct((TOK + 16, LATS), F32),
            jax.ShapeDtypeStruct((GROUP * TOK, LATS), BF16),
            jax.ShapeDtypeStruct((GROUP, 128, 128), jnp.int32),
        ),
        in_specs=[VMEM, ANY, VMEM, VMEM],
        out_specs=(VMEM, VMEM, VMEM, VMEM),
        scratch_shapes=[
            pltpu.VMEM((4, 256, D), BF16),
            pltpu.SemaphoreType.DMA((4,)),
            pltpu.SemaphoreType.DMA((7,)),
            pltpu.SemaphoreType.DMA((7,)),
            pltpu.SemaphoreType.DMA((7,)),
            pltpu.SemaphoreType.DMA((7,)),
            pltpu.SemaphoreType.DMA((2,)),
            pltpu.SemaphoreType.DMA((2,)),
            pltpu.SemaphoreType.DMA((2,)),
        ],
        compiler_params=pltpu.CompilerParams(
            collective_id=0, has_side_effects=True, vmem_limit_bytes=48 * 1024 * 1024
        ),
        name="opening",
    )(act, dictionary, act8, ids)


def slots_of(read, ids, first):
    def rows(row):
        local = ids[pl.ds(row, 8), :] - first
        inside = (local >= 0) & (local < LATS)
        code = jnp.where(inside, local, 8 * 128)
        low, high = code & 127, code >> 7
        second = lax.broadcasted_iota(jnp.int32, (8, 128), 1) >= SLOTS
        total = jnp.zeros((8, 128), F32)
        for c in range(8):
            one = jnp.take_along_axis(read(row, c), low, axis=1)
            two = jnp.take_along_axis(read(row + 128, c), low, axis=1)
            total = jnp.where(high == c, jnp.where(second, two, one), total)
        return total

    return rows


def pick_kernel(first_ref, value_ref, ids_ref, out_ref):
    first = first_ref[0]

    def step(block, carry):
        row = pl.multiple_of(block * 16, 16)
        halves = []
        for part in range(2):
            at = pl.multiple_of(row + part * 8, 8)
            rows = slots_of(
                lambda r, c: value_ref[pl.ds(r, 8), c * 128 : (c + 1) * 128], ids_ref, first
            )
            halves.append(rows(at))
        out_ref[pl.ds(row, 16), :] = jnp.concatenate(halves, axis=0).astype(BF16)
        return carry

    lax.fori_loop(0, 8, step, 0)


def pick(first, values, ids):
    return pl.pallas_call(
        pick_kernel,
        out_shape=jax.ShapeDtypeStruct((128, 128), BF16),
        in_specs=[pl.BlockSpec(memory_space=pltpu.SMEM), VMEM, VMEM],
        out_specs=VMEM,
        name="pick",
    )(first, values, ids)


def sum_kernel(
    part_ref, act_ref, res8_ref,
    half, down_out, down_in, up_out, up_in, own_sum, other_sum, res, slices,
    half_sem, dsend, drecv, usend, urecv, xsend, xrecv, asend, arecv,
    gdsend, gdrecv, gusend, gurecv, csend, crecv, own_sem,
):
    me = seat()
    core = lax.axis_index("lat_2")
    z = lax.axis_index("lat_1")
    x = lax.axis_index("lat_0")
    other_core = {"lat_2": 1 - core}
    below = {"lat_1": lax.rem(z + 7, 8)}
    above = {"lat_1": lax.rem(z + 1, 8)}
    other_x = {"lat_0": 1 - x}
    enter([other_core, below, above, other_x] + group_partners())
    sends = []

    def start(copy):
        copy.start()
        sends.append(copy)

    give = pl.multiple_of((1 - core) * 128, 128)
    keep = pl.multiple_of(core * 128, 128)
    copy = remote(
        part_ref.at[pl.ds(give, 128)], half, half_sem.at[0], half_sem.at[1], other_core
    )
    start(copy)
    copy.wait_recv()
    width = D // PIECES

    def mine(chunk, h):
        cols = slice(h * width, (h + 1) * width)
        at = pl.multiple_of(chunk * 16, 16)
        return part_ref[pl.ds(keep + at, 16), cols].astype(F32) + half[pl.ds(at, 16), cols].astype(
            F32
        )

    for s in range(1, 6):
        for h in range(PIECES):
            cols = pl.ds(h * width, width)
            if s <= 4:
                value = mine(lax.rem(z + 8 - (5 - s), 8), h)
                if s > 1:
                    drecv_copy = pltpu.make_async_copy(
                        down_in.at[s - 2, :, cols], down_in.at[s - 2, :, cols], drecv.at[s - 2, h]
                    )
                    drecv_copy.wait()
                    value = value + down_in[s - 2, :, h * width : (h + 1) * width].astype(F32)
                down_out[s - 1, :, h * width : (h + 1) * width] = value.astype(BF16)
                start(
                    remote(
                        down_out.at[s - 1, :, cols],
                        down_in.at[s - 1, :, cols],
                        dsend.at[s - 1, h],
                        drecv.at[s - 1, h],
                        below,
                    )
                )
            if s <= 3:
                value = mine(lax.rem(z + (4 - s), 8), h)
                if s > 1:
                    pltpu.make_async_copy(
                        up_in.at[s - 2, :, cols], up_in.at[s - 2, :, cols], urecv.at[s - 2, h]
                    ).wait()
                    value = value + up_in[s - 2, :, h * width : (h + 1) * width].astype(F32)
                up_out[s - 1, :, h * width : (h + 1) * width] = value.astype(BF16)
                start(
                    remote(
                        up_out.at[s - 1, :, cols],
                        up_in.at[s - 1, :, cols],
                        usend.at[s - 1, h],
                        urecv.at[s - 1, h],
                        above,
                    )
                )
            if s == 5:
                pltpu.make_async_copy(
                    down_in.at[3, :, cols], down_in.at[3, :, cols], drecv.at[3, h]
                ).wait()
                pltpu.make_async_copy(
                    up_in.at[2, :, cols], up_in.at[2, :, cols], urecv.at[2, h]
                ).wait()
                at = slice(h * width, (h + 1) * width)
                total = mine(z, h) + down_in[3, :, at].astype(F32) + up_in[2, :, at].astype(F32)
                own_sum[:, at] = total.astype(BF16)
                start(
                    remote(
                        own_sum.at[:, cols],
                        other_sum.at[:, cols],
                        xsend.at[h],
                        xrecv.at[h],
                        other_x,
                    )
                )
    rows = pl.multiple_of(keep + z * 16, 16)
    for h in range(PIECES):
        cols = pl.ds(h * width, width)
        at = slice(h * width, (h + 1) * width)
        pltpu.make_async_copy(other_sum.at[:, cols], other_sum.at[:, cols], xrecv.at[h]).wait()
        res[:, at] = (own_sum[:, at].astype(F32) + other_sum[:, at].astype(F32)) - act_ref[
            pl.ds(rows, 16), at
        ].astype(F32)
    for j in range(GROUP):
        slices[j] = res[:, j * OWN : (j + 1) * OWN].astype(BF16)
    for delta in range(1, GROUP):
        j, device = peer(delta)
        start(
            remote(
                slices.at[j],
                res8_ref.at[me, pl.ds(rows, 16)],
                asend.at[delta - 1],
                arecv.at[delta - 1],
                device,
            )
        )
    own = pltpu.make_async_copy(slices.at[me], res8_ref.at[me, pl.ds(rows, 16)], own_sem)
    own.start()
    own.wait()
    for delta in range(1, GROUP):
        j = peer_from(delta)
        pltpu.make_async_copy(
            res8_ref.at[j, pl.ds(rows, 16)], res8_ref.at[j, pl.ds(rows, 16)], arecv.at[delta - 1]
        ).wait()

    def region(chunk, h):
        at = pl.multiple_of(keep + chunk * 16, 16)
        return res8_ref.at[pl.ds(h * 2, 2), pl.ds(at, 16)]

    def chunk_rows(base, chunk):
        at = pl.multiple_of(base + chunk * 16, 16)
        return res8_ref.at[:, pl.ds(at, 16)]

    def to_core(chunk, n):
        start(
            remote(
                chunk_rows(keep, chunk), chunk_rows(keep, chunk), csend.at[n], crecv.at[n], other_core
            )
        )

    for s in range(1, 6):
        for h in range(4):
            if s <= 4:
                chunk = lax.rem(z + s - 1, 8)
                if s > 1:
                    pltpu.make_async_copy(
                        region(chunk, h), region(chunk, h), gdrecv.at[s - 2, h]
                    ).wait()
                start(
                    remote(
                        region(chunk, h),
                        region(chunk, h),
                        gdsend.at[s - 1, h],
                        gdrecv.at[s - 1, h],
                        below,
                    )
                )
            else:
                chunk = lax.rem(z + 4, 8)
                pltpu.make_async_copy(region(chunk, h), region(chunk, h), gdrecv.at[3, h]).wait()
            if s <= 4:
                chunk = lax.rem(z + 8 - (s - 1), 8)
                if s > 1:
                    pltpu.make_async_copy(
                        region(chunk, h), region(chunk, h), gurecv.at[s - 2, h]
                    ).wait()
                if s <= 3:
                    start(
                        remote(
                            region(chunk, h),
                            region(chunk, h),
                            gusend.at[s - 1, h],
                            gurecv.at[s - 1, h],
                            above,
                        )
                    )
        to_core(lax.rem(z + s - 1, 8), s - 1)
        if 2 <= s <= 4:
            to_core(lax.rem(z + 8 - (s - 1), 8), 3 + s)
    for n in range(8):
        chunk = lax.rem(z + n, 8) if n < 5 else lax.rem(z + 8 - (n - 4), 8)
        there = pl.multiple_of(give, 128)
        pltpu.make_async_copy(
            chunk_rows(there, chunk), chunk_rows(there, chunk), crecv.at[n]
        ).wait()
    for copy in sends:
        copy.wait_send()


def summed(part, act):
    dma = pltpu.SemaphoreType.DMA
    return pl.pallas_call(
        sum_kernel,
        out_shape=jax.ShapeDtypeStruct((GROUP, TOK, OWN), BF16),
        in_specs=[VMEM, VMEM],
        out_specs=VMEM,
        scratch_shapes=[
            pltpu.VMEM((128, D), BF16),
            pltpu.VMEM((4, 16, D), BF16),
            pltpu.VMEM((4, 16, D), BF16),
            pltpu.VMEM((3, 16, D), BF16),
            pltpu.VMEM((3, 16, D), BF16),
            pltpu.VMEM((16, D), BF16),
            pltpu.VMEM((16, D), BF16),
            pltpu.VMEM((16, D), F32),
            pltpu.VMEM((GROUP, 16, OWN), BF16),
            dma((2,)),
            dma((4, PIECES)),
            dma((4, PIECES)),
            dma((3, PIECES)),
            dma((3, PIECES)),
            dma((PIECES,)),
            dma((PIECES,)),
            dma((7,)),
            dma((7,)),
            dma((4, 4)),
            dma((4, 4)),
            dma((3, 4)),
            dma((3, 4)),
            dma((8,)),
            dma((8,)),
            dma,
        ],
        compiler_params=pltpu.CompilerParams(
            collective_id=1, has_side_effects=True, vmem_limit_bytes=32 * 1024 * 1024
        ),
        name="summed",
    )(part, act)


def grads_kernel(first_ref, res_ref, dict_ref, ids_ref, out_ref, dense):
    first = first_ref[0]
    dense[...] = lax.dot_general(
        res_ref[0], dict_ref[...], (((1,), (1,)), ((), ())), preferred_element_type=F32
    )

    def step(block, carry):
        row = pl.multiple_of(block * 16, 16)
        halves = []
        for part in range(2):
            at = pl.multiple_of(row + part * 8, 8)
            rows = slots_of(
                lambda r, c: dense[pl.ds(r, 8), c * 128 : (c + 1) * 128], ids_ref.at[0], first
            )
            halves.append(rows(at))
        out_ref[0, pl.ds(row, 16), :] = jnp.concatenate(halves, axis=0).astype(BF16)
        return carry

    lax.fori_loop(0, 8, step, 0)


def grads(first, res8, dict_own, ids8):
    return pl.pallas_call(
        grads_kernel,
        grid=(GROUP,),
        out_shape=jax.ShapeDtypeStruct((GROUP, 128, 128), BF16),
        in_specs=[
            pl.BlockSpec(memory_space=pltpu.SMEM),
            pl.BlockSpec((1, TOK, OWN), lambda i: (i, 0, 0)),
            pl.BlockSpec((LATS, OWN), lambda i: (0, 0)),
            pl.BlockSpec((1, 128, 128), lambda i: (i, 0, 0)),
        ],
        out_specs=pl.BlockSpec((1, 128, 128), lambda i: (i, 0, 0)),
        scratch_shapes=[pltpu.VMEM((TOK, LATS), F32)],
        name="grads",
    )(first, res8, dict_own, ids8)


def codes_kernel(
    part_ref, codes_ref, total_ref, codes8_ref,
    arrived, own_total, psend, precv, csend, crecv, tsend, trecv, own_sem,
):
    me = seat()
    enter(group_partners())
    sends = []
    for delta in range(1, GROUP):
        j, device = peer(delta)
        copy = remote(
            part_ref.at[j], arrived.at[me], psend.at[delta - 1], precv.at[delta - 1], device
        )
        copy.start()
        sends.append(copy)
    for delta in range(1, GROUP):
        _, device = peer(delta)
        copy = remote(
            codes_ref, codes8_ref.at[me], csend.at[delta - 1], crecv.at[delta - 1], device
        )
        copy.start()
        sends.append(copy)
    own = pltpu.make_async_copy(part_ref.at[me], arrived.at[me], own_sem.at[0])
    own_codes = pltpu.make_async_copy(codes_ref, codes8_ref.at[me], own_sem.at[1])
    own.start()
    own_codes.start()
    own.wait()
    for delta in range(1, GROUP):
        pltpu.make_async_copy(part_ref.at[0], arrived.at[0], precv.at[delta - 1]).wait()
    total = arrived[0].astype(F32)
    for j in range(1, GROUP):
        total = total + arrived[j].astype(F32)
    own_total[...] = total.astype(BF16)
    for delta in range(1, GROUP):
        _, device = peer(delta)
        copy = remote(
            own_total, total_ref.at[me], tsend.at[delta - 1], trecv.at[delta - 1], device
        )
        copy.start()
        sends.append(copy)
    own_codes.wait()
    own = pltpu.make_async_copy(own_total, total_ref.at[me], own_sem.at[0])
    own.start()
    own.wait()
    for delta in range(1, GROUP):
        pltpu.make_async_copy(codes_ref, codes8_ref.at[0], crecv.at[delta - 1]).wait()
        pltpu.make_async_copy(own_total, total_ref.at[0], trecv.at[delta - 1]).wait()
    for copy in sends:
        copy.wait_send()


def all_codes(parts, codes):
    shape = jax.ShapeDtypeStruct((GROUP, 128, 128), BF16)
    return pl.pallas_call(
        codes_kernel,
        out_shape=(shape, shape),
        in_specs=[VMEM, VMEM],
        out_specs=(VMEM, VMEM),
        scratch_shapes=[
            pltpu.VMEM((GROUP, 128, 128), BF16),
            pltpu.VMEM((128, 128), BF16),
        ]
        + [pltpu.SemaphoreType.DMA((7,))] * 6
        + [pltpu.SemaphoreType.DMA((2,))],
        compiler_params=pltpu.CompilerParams(
            collective_id=2, has_side_effects=True, vmem_limit_bytes=16 * 1024 * 1024
        ),
        name="all_codes",
    )(parts, codes)


SEQ_ROWS = 4 * TOK + 16


def dictionary_kernel(
    where_ref, inv_ref, codes_ref, grad_ref, res_ref, act_ref, taps_ref, lat_ref,
    out_ref, small_ref, dense, pre, grad_in,
):
    width = inv_ref.shape[1]
    tiles = width // 128
    for b in range(2):
        pre[b, 0:8, :] = jnp.zeros((8, width), F32)
        pre[b, 8 + 4 * TOK :, :] = jnp.zeros((8, width), F32)
    keep = lax.broadcasted_iota(jnp.int32, (16, 128), 1) < SLOTS

    def expand(block, carry):
        j = block // 8
        row = pl.multiple_of(lax.rem(block, 8) * 16, 16)
        codes = codes_ref[j, pl.ds(row, 16), :].astype(F32)
        grad = grad_ref[j, pl.ds(row, 16), :].astype(F32)
        for side in range(2):
            if side:
                codes = pltpu.roll(codes, SLOTS, 1)
                grad = pltpu.roll(grad, SLOTS, 1)
            codes_side = jnp.where(keep, codes, 0.0)
            grad_side = jnp.where(keep, grad, 0.0)
            start = pl.multiple_of(j * TOK + side * 128 + row, 16)
            into = pl.multiple_of(8 + (j // 2) * TOK + side * 128 + row, 8)
            for c in range(tiles):
                at = slice(c * 128, (c + 1) * 128)
                slot = inv_ref[pl.ds(start, 16), at].astype(F32).astype(jnp.int32)
                wide = [
                    jnp.take_along_axis(codes_side[r : r + 8], slot[r : r + 8], axis=1)
                    for r in (0, 8)
                ]
                dense[pl.ds(start, 16), at] = jnp.concatenate(wide, axis=0).astype(BF16)
                for r in (0, 8):
                    pre[lax.rem(j, 2), pl.ds(into + r, 8), at] = jnp.take_along_axis(
                        grad_side[r : r + 8], slot[r : r + 8], axis=1
                    )
        return carry

    lax.fori_loop(0, 64, expand, 0)

    def spread(block, carry):
        b, row = block // 16, lax.rem(block, 16) * 64
        near = pre[b, pl.ds(pl.multiple_of(row, 8), 80), :]
        total = jnp.zeros((64, width), F32)
        for k in range(TAPS):
            begin = 8 + HALF - k
            total = total + taps_ref[k : k + 1, :] * near[begin : begin + 64]
        j = (row // TOK) * 2 + b
        into = pl.multiple_of(j * TOK + lax.rem(row, TOK), 64)
        grad_in[pl.ds(into, 64), :] = total.astype(BF16)
        return carry

    lax.fori_loop(0, 32, spread, 0)
    out_ref[...] = lax.dot_general(
        dense[...], res_ref[...], (((0,), (0,)), ((), ())), preferred_element_type=F32
    ) + lax.dot_general(
        grad_in[...], act_ref[...], (((0,), (0,)), ((), ())), preferred_element_type=F32
    )
    own = pre[where_ref[1], pl.ds(pl.multiple_of(8 + where_ref[0] * TOK, 8), TOK), :]
    for k in range(TAPS):
        small_ref[k : k + 1, :] = jnp.sum(
            own * lat_ref[k + HALF : k + HALF + TOK, :], axis=0, keepdims=True
        )
    small_ref[TAPS : TAPS + 1, :] = jnp.sum(own, axis=0, keepdims=True)
    small_ref[TAPS + 1 :, :] = jnp.zeros((16 - TAPS - 1, width), F32)


def dictionary_gradient(where, inv, codes8, grad8, res, cols, taps, lat):
    width = 256
    return pl.pallas_call(
        dictionary_kernel,
        grid=(LATS // width,),
        out_shape=(
            jax.ShapeDtypeStruct((LATS, OWN), F32),
            jax.ShapeDtypeStruct((16, LATS), F32),
        ),
        in_specs=[
            pl.BlockSpec(memory_space=pltpu.SMEM),
            pl.BlockSpec((GROUP * TOK, width), lambda i: (0, i)),
            pl.BlockSpec((GROUP, 128, 128), lambda i: (0, 0, 0)),
            pl.BlockSpec((GROUP, 128, 128), lambda i: (0, 0, 0)),
            pl.BlockSpec((GROUP * TOK, OWN), lambda i: (0, 0)),
            pl.BlockSpec((GROUP * TOK, OWN), lambda i: (0, 0)),
            pl.BlockSpec((TAPS, width), lambda i: (0, i)),
            pl.BlockSpec((TOK + 16, width), lambda i: (0, i)),
        ],
        out_specs=(
            pl.BlockSpec((width, OWN), lambda i: (i, 0)),
            pl.BlockSpec((16, width), lambda i: (0, i)),
        ),
        scratch_shapes=[
            pltpu.VMEM((GROUP * TOK, width), BF16),
            pltpu.VMEM((2, SEQ_ROWS, width), F32),
            pltpu.VMEM((GROUP * TOK, width), BF16),
        ],
        name="dictionary_gradient",
    )(where, inv, codes8, grad8, res, cols, taps, lat)


def small_kernel(part_ref, out_ref, arrived, send, recv):
    me = seat()
    enter(group_partners())
    sends = []
    for delta in range(1, GROUP):
        _, device = peer(delta)
        copy = remote(part_ref, arrived.at[me], send.at[delta - 1], recv.at[delta - 1], device)
        copy.start()
        sends.append(copy)
    arrived[me] = part_ref[...]
    for delta in range(1, GROUP):
        pltpu.make_async_copy(part_ref, arrived.at[0], recv.at[delta - 1]).wait()
    total = arrived[0]
    for j in range(1, GROUP):
        total = total + arrived[j]
    out_ref[...] = total
    for copy in sends:
        copy.wait_send()


def small_sum(part):
    return pl.pallas_call(
        small_kernel,
        out_shape=jax.ShapeDtypeStruct((16, LATS), F32),
        in_specs=[VMEM],
        out_specs=VMEM,
        scratch_shapes=[
            pltpu.VMEM((GROUP, 16, LATS), F32),
            pltpu.SemaphoreType.DMA((7,)),
            pltpu.SemaphoreType.DMA((7,)),
        ],
        compiler_params=pltpu.CompilerParams(
            collective_id=3, has_side_effects=True, vmem_limit_bytes=16 * 1024 * 1024
        ),
        name="small_sum",
    )(part)


def body(activations, dictionary, topk_ids, kernel_taps, enc_bias):
    act = activations[0]
    ids = topk_ids[0]
    ids = jnp.concatenate([ids[:128], ids[128:]], axis=1)
    me = seat()
    first = (lax.axis_index(LAT) * LATS).astype(jnp.int32)[None]
    act8 = act.reshape(TOK, GROUP, OWN).swapaxes(0, 1)
    cols, lat, inv, ids8 = opening(act, dictionary, act8, ids)
    preact = jnp.zeros((TOK, LATS), F32)
    for k in range(TAPS):
        preact = preact + kernel_taps[k][None, :] * lat[k + HALF : k + HALF + TOK]
    preact = preact + enc_bias[None, :]
    own_inv = lax.dynamic_slice_in_dim(inv, me * TOK, TOK, axis=0)
    latents = jnp.where(own_inv < NONE, preact, 0.0).astype(BF16)
    part = jnp.einsum("tl,ld->td", latents, dictionary, preferred_element_type=F32).astype(BF16)
    codes = pick(first, latents.astype(F32), ids)
    res8 = summed(part, act)
    dict_own = lax.dynamic_slice_in_dim(dictionary, me * OWN, OWN, axis=1)
    parts = grads(first, res8, dict_own, ids8)
    grad8, codes8 = all_codes(parts, codes)
    where = jnp.stack([lax.axis_index("seq"), lax.axis_index("batch")]).astype(jnp.int32)
    grad_dictionary, small = dictionary_gradient(
        where,
        inv,
        codes8,
        grad8,
        res8.reshape(GROUP * TOK, OWN),
        cols.reshape(GROUP * TOK, OWN),
        kernel_taps,
        lat,
    )
    small = small_sum(small)
    return grad_dictionary, small[:TAPS], small[TAPS]


def solution(mesh):
    finer = Mesh(
        mesh.devices.reshape(mesh.shape["seq"], 2, 8, 2, mesh.shape["batch"]),
        ("seq", "lat_0", "lat_1", "lat_2", "batch"),
    )
    return jax.shard_map(
        body,
        mesh=finer,
        in_specs=(
            P("batch", "seq", None),
            P(LAT, None),
            P("batch", "seq", None),
            P(None, LAT),
            P(LAT),
        ),
        out_specs=(P(LAT, ("seq", "batch")), P(None, LAT), P(LAT)),
        check_vma=False,
    )
```

time: 318 us -> 231 us (0.73)
  Pallas kernels: 0 us -> 200 us
  waiting for transfers between devices: 139 us -> 0 us
  blocking collectives: 77.1 us -> 0 us
  matrix products: 30.1 us -> 5.16 us
  starting transfers between devices: 19.8 us -> 0 us
  between operations: 14.4 us -> 0.78 us
  other arithmetic: 15.7 us -> 4.34 us
    pallas_call x0 -> x7, Pallas kernels: none -> 200 us  [the longest x1 61.9 us: dictionary_gradient(): pl.pallas_call(dictionary_kernel, grid=(LATS // width,), out_shape=(jax.S...]
    unnamed x2 -> x0, waiting for transfers between devices: 123 us -> none
    all_to_all x4 -> x0, blocking collectives: 77.1 us -> none  [the longest x1 36.7 us: summed_rows(): lax.all_to_all(nearer.astype(jnp.bfloat16), far, split_axis=0, concat_axi...]
    dot_general x5 -> x1, matrix products: 30.1 us -> 5.16 us  [body(): jnp.einsum('tl,ld->td', latents, dictionary, preferred_element_type=F32)]
    all_to_all x2 -> x0, waiting for transfers between devices: 15.9 us -> none  [copy_for_each(): lax.all_to_all(jnp.broadcast_to(shard[None], (devices, *shard.shape)), ax...]
    ppermute x4 -> x0, starting transfers between devices: 11.9 us -> none  [the longest x2 9.27 us: extended(): lax.ppermute(tail, axis, [(i, (i + 1) % count) for i in range(ends)])]
    reduce_or x1 -> x0, other arithmetic: 9.43 us -> none  [body(): jnp.any(chosen_ids[:, :, None] == latent_ids[None, None, :], axis=1)]
    unnamed x19 -> x29, local copies, waits for them, and re-layouts: 17.8 us -> 9.65 us
  transfers between devices with their start and end apart: 7 -> 0, of which waited for: 3 -> 0; matrix products, arithmetic and copies ran while one was open for 7% -> 0% of each run, Pallas kernels for 0% -> 0%
where the time goes in v1:
time: 231 us; the launch traced here: 230 us
  Pallas kernels  200 us (87%)
  local copies, waits for them, and re-layouts  18.9 us (8%)
  matrix products  5.16 us (2%)
  other arithmetic  4.34 us (2%)
    pallas_call x1, Pallas kernels, dictionary_gradient(): pl.pallas_call(dictionary_kernel, grid=(LATS // width,), out_shape=(jax.S...  61.9 us
    pallas_call x1, Pallas kernels, opening(): pl.pallas_call(opening_kernel, out_shape=(jax.ShapeDtypeStruct((GROUP, TO...  54.7 us
    pallas_call x1, Pallas kernels, summed(): pl.pallas_call(sum_kernel, out_shape=jax.ShapeDtypeStruct((GROUP, TOK, OW...  45 us
    pallas_call x1, Pallas kernels, all_codes(): pl.pallas_call(codes_kernel, out_shape=(shape, shape), in_specs=[VMEM, VM...  14.7 us
    pallas_call x1, Pallas kernels, grads(): pl.pallas_call(grads_kernel, grid=(GROUP,), out_shape=jax.ShapeDtypeStruc...  12.3 us
    unnamed x29, local copies, waits for them, and re-layouts  9.65 us
    pallas_call x1, Pallas kernels, small_sum(): pl.pallas_call(small_kernel, out_shape=jax.ShapeDtypeStruct((16, LATS), F...  9.36 us
    dot_general x1, matrix products, body(): jnp.einsum('tl,ld->td', latents, dictionary, preferred_element_type=F32)  5.16 us

profile of v1, /device:TPU:32, one launch (start us, length us, event | category | flops | bytes accessed | tf_op | source)
XLA Modules:
  0.0 229.6 jit_solution(6162209161127293021)
XLA Ops:
  0.6 0.0 copy-start.2
  0.7 0.6 pad_add_fusion.1.where_ref
  1.2 1.2 fusion.1
  2.4 0.8 fusion.2
  3.2 0.1 copy.16
  3.3 0.1 copy.17
  3.4 0.1 pad_add_fusion.ids_ref
  3.5 0.0 copy-start.5
  3.5 2.9 %constant_dynamic-slice_fusion.dict_ref = bf16[1024,448]{1,0:T(8,128)(2,1)} fusion(bf16[1024,3584]{1,0:T(8,128)(2,1)} %dict_ref.1, s32[]{:T(128)S(6)} %select_n.12), kind=kLoop, calls=%fused_computation.4 | loop fusion | bytes 1835012 | tf_op jit(solution)/shard_map/dynamic_slice | solution.py:728
  6.4 0.0 copy-done.2
  6.4 2.2 copy.11
  8.7 3.8 %copy.12 = bf16[256,8,448]{2,0,1:T(8,128)(2,1)} copy(bf16[256,8,448]{0,2,1:T(8,128)(2,1)} %bitcast.29) | data formatting | bytes 3670016 | tf_op jit(solution)/shard_map/reshape;squeeze | solution.py:717
  12.5 0.0 copy-done.5
  12.5 54.7 %opening.1 = (bf16[8,256,448]{2,1,0:T(8,128)(2,1)S(1)}, f32[272,1024]{1,0:T(8,128)S(1)}, bf16[2048,1024]{1,0:T(8,128)(2,1)}, s32[8,128,128]{2,1,0:T(8,128)S(1)}) custom-call(bf16[256,3584]{1,0:T(8,128)(2,1)S(1)} %bitcast.24, bf16[1024,3584]{1,0:T(8,128)(2,1)} %dict_ref.1, bf16[8,256,448]{2,1,0:T(8,128)(2,1)} %bitcast.28, s32[128,128]{1,0:T(8,128)S(1)} %pad_add_fusion.ids_ref), custom_call_target="tpu_custom_call" | custom-call | tf_op jit(solution)/shard_map/opening/pallas_call | solution.py:161
  67.2 0.0 copy-start
  67.2 0.0 copy-start.3
  67.2 3.7 %fusion = (f32[256,1024]{1,0:T(8,128)}, bf16[256,1024]{1,0:T(8,128)(2,1)S(1)}) fusion(f32[1024]{0:T(1024)S(1)} %copy-done.11, f32[272,1024]{1,0:T(8,128)S(1)} %get-tuple-element.12.lat_ref, f32[1024]{0:T(1024)S(1)} %bitcast.40, f32[1024]{0:T(1024)S(1)} %bitcast.33, f32[1024]{0:T(1024)S(1)} %bitcast.34, f32[1024]{0:T(1024)S(1)} %bitcast.35, ...), kind=kLoop, calls=%fused_computation.5 | loop fusion | flops 6291456 | bytes 11575300 | tf_op jit(solution)/shard_map/convert_element_type | solution.py:726
  70.9 2.6 %pick.1.codes_ref = bf16[128,128]{1,0:T(8,128)(2,1)} custom-call(s32[1]{0:T(128)} %bitcast.7.first_ref, f32[256,1024]{1,0:T(8,128)} %get-tuple-element.25.value_ref, s32[128,128]{1,0:T(8,128)} %copy-done.5), custom_call_target="tpu_custom_call" | custom-call | tf_op jit(solution)/shard_map/pick/pallas_call | solution.py:225
  73.5 5.2 %convolution_convert_fusion.part_ref = bf16[256,3584]{1,0:T(8,128)(2,1)S(1)} fusion(bf16[256,1024]{1,0:T(8,128)(2,1)S(1)} %get-tuple-element.26, bf16[1024,3584]{1,0:T(8,128)(2,1)} %dict_ref.1), kind=kOutput, calls=%fused_computation | convolution fusion | flops 1879965696 | bytes 9699328 | tf_op jit(solution)/shard_map/tl,ld->td/dot_general | solution.py:725
  78.7 45.0 %summed.1.res_ref = bf16[8,256,448]{2,1,0:T(8,128)(2,1)S(1)} custom-call(bf16[256,3584]{1,0:T(8,128)(2,1)S(1)} %convolution_convert_fusion.part_ref, bf16[256,3584]{1,0:T(8,128)(2,1)S(1)} %bitcast.25), custom_call_target="tpu_custom_call" | custom-call | tf_op jit(solution)/shard_map/summed/pallas_call | solution.py:424
  123.6 0.0 copy-start.1
  123.7 1.3 copy-done.1
  125.0 12.3 %grads.1.part_ref = bf16[8,128,128]{2,1,0:T(8,128)(2,1)} custom-call(s32[1]{0:T(128)} %bitcast.7.first_ref, bf16[8,256,448]{2,1,0:T(8,128)(2,1)} %copy-done.1, bf16[1024,448]{1,0:T(8,128)(2,1)} %constant_dynamic-slice_fusion.dict_ref, s32[8,128,128]{2,1,0:T(8,128)} %copy-done.6), custom_call_target="tpu_custom_call" | custom-call | tf_op jit(solution)/shard_map/grads/pallas_call | solution.py:485
  137.3 0.9 copy-done.4
  138.2 14.7 %all_codes.1 = (bf16[8,128,128]{2,1,0:T(8,128)(2,1)S(1)}, bf16[8,128,128]{2,1,0:T(8,128)(2,1)S(1)}) custom-call(bf16[8,128,128]{2,1,0:T(8,128)(2,1)S(1)} %copy-done.4, bf16[128,128]{1,0:T(8,128)(2,1)S(1)} %copy-done.9), custom_call_target="tpu_custom_call" | custom-call | tf_op jit(solution)/shard_map/all_codes/pallas_call | solution.py:553
  152.9 0.7 copy-done.7
  153.6 0.7 copy-done.8
  154.3 61.9 %dictionary_gradient.1 = (f32[1024,448]{1,0:T(8,128)}, f32[16,1024]{1,0:T(8,128)}) custom-call(s32[2]{0:T(128)} %pad_add_fusion.1.where_ref, bf16[2048,1024]{1,0:T(8,128)(2,1)} %get-tuple-element.11.inv_ref, bf16[8,128,128]{2,1,0:T(8,128)(2,1)} %copy-done.8, bf16[8,128,128]{2,1,0:T(8,128)(2,1)} %copy-done.7, bf16[2048,448]{1,0:T(8,128)(2,1)} %bitcast.23, ...), custom_call_target="tpu_custom_call" | custom-call | tf_op jit(solution)/shard_map/dictionary_gradient/pallas_call | solution.py:643
  216.2 2.8 %copy.15 = f32[1024,448]{0,1:T(8,128)} copy(f32[1024,448]{1,0:T(8,128)} %get-tuple-element.22) | data formatting | bytes 3670016
  219.0 9.4 %small_sum.1 = f32[16,1024]{1,0:T(8,128)S(1)} custom-call(f32[16,1024]{1,0:T(8,128)S(1)} %copy-done.10), custom_call_target="tpu_custom_call" | custom-call | tf_op jit(solution)/shard_map/small_sum/pallas_call | solution.py:694
  228.4 0.6 slice.95
  229.0 0.6 copy.19
  (13 shorter events, 0.0 us)
Async XLA Ops:
  0.6 5.8 %copy-start.2 = (bf16[1,256,3584]{2,1,0:T(8,128)(2,1)S(1)}, bf16[1,256,3584]{2,1,0:T(8,128)(2,1)}, u32[]{:S(2)}) copy-start(bf16[1,256,3584]{2,1,0:T(8,128)(2,1)} %param.5) | copy-start | bytes 5505028
  3.5 9.0 %copy-start.5 = (s32[128,128]{1,0:T(8,128)}, s32[128,128]{1,0:T(8,128)S(1)}, u32[]{:S(2)}) copy-start(s32[128,128]{1,0:T(8,128)S(1)} %pad_add_fusion.ids_ref) | copy-start | bytes 196612
  12.5 54.7 %copy-start.11 = (f32[1024]{0:T(1024)S(1)}, f32[1024]{0:T(1024)}, u32[]{:S(2)}) copy-start(f32[1024]{0:T(1024)} %param.9) | copy-start | bytes 12292
  67.2 3.7 %copy-start = (f32[272,1024]{1,0:T(8,128)}, f32[272,1024]{1,0:T(8,128)S(1)}, u32[]{:S(2)}) copy-start(f32[272,1024]{1,0:T(8,128)S(1)} %get-tuple-element.12.lat_ref) | copy-start | bytes 3342340
  67.2 3.7 %copy-start.3 = (bf16[8,256,448]{2,1,0:T(8,128)(2,1)}, bf16[8,256,448]{2,1,0:T(8,128)(2,1)S(1)}, u32[]{:S(2)}) copy-start(bf16[8,256,448]{2,1,0:T(8,128)(2,1)S(1)} %get-tuple-element.16) | copy-start | bytes 5505028
  67.2 3.7 %copy-start.6 = (s32[8,128,128]{2,1,0:T(8,128)}, s32[8,128,128]{2,1,0:T(8,128)S(1)}, u32[]{:S(2)}) copy-start(s32[8,128,128]{2,1,0:T(8,128)S(1)} %get-tuple-element.13.ids_ref) | copy-start | bytes 1572868
  123.6 1.4 copy-start.1
  125.0 12.3 %copy-start.9 = (bf16[128,128]{1,0:T(8,128)(2,1)S(1)}, bf16[128,128]{1,0:T(8,128)(2,1)}, u32[]{:S(2)}) copy-start(bf16[128,128]{1,0:T(8,128)(2,1)} %pick.1.codes_ref) | copy-start | bytes 98308
  137.3 1.0 copy-start.4
  152.9 0.7 copy-start.7
  153.6 0.7 copy-start.8
  216.2 2.8 %copy-start.10 = (f32[16,1024]{1,0:T(8,128)S(1)}, f32[16,1024]{1,0:T(8,128)}, u32[]{:S(2)}) copy-start(f32[16,1024]{1,0:T(8,128)} %get-tuple-element.18.part_ref) | copy-start | bytes 196612

commit v2 on v0

v2 whole, which is shorter than its diff:
```python
import functools

import jax
import jax.numpy as jnp
from jax import lax
from jax.experimental import pallas as pl
from jax.experimental.pallas import tpu as pltpu
from jax.sharding import Mesh
from jax.sharding import PartitionSpec as P

TAPS = 9
HALF = 4
LAT = ("lat_0", "lat_1", "lat_2")
D = 3584
TOK = 256
LATS = 1024
SLOTS = 64
OWN = 448
WIN = 512
GROUP = 8
NONE = 64
PIECES = 4
F32 = jnp.float32
BF16 = jnp.bfloat16
MESH = pl.DeviceIdType.MESH
VMEM = pl.BlockSpec(memory_space=pltpu.VMEM)
ANY = pl.BlockSpec(memory_space=pl.ANY)
BIG = 64 * 1024 * 1024 - 65536


def seat():
    return lax.axis_index("seq") * 2 + lax.axis_index("batch")


def peer(delta):
    j = lax.rem(seat() + delta, GROUP)
    return j, {"seq": j // 2, "batch": lax.rem(j, 2)}


def peer_from(delta):
    return lax.rem(seat() + GROUP - delta, GROUP)


def enter(partners):
    barrier = pltpu.get_barrier_semaphore()
    for device in partners:
        pl.semaphore_signal(barrier, inc=1, device_id=device, device_id_type=MESH)
    pl.semaphore_wait(barrier, len(partners))


def group_partners():
    return [peer(delta)[1] for delta in range(1, GROUP)]


def remote(src, dst, send_sem, recv_sem, device):
    return pltpu.make_async_remote_copy(
        src_ref=src,
        dst_ref=dst,
        send_sem=send_sem,
        recv_sem=recv_sem,
        device_id=device,
        device_id_type=MESH,
    )


def first_latent():
    group = lax.axis_index("lat_0") * 16 + lax.axis_index("lat_1") * 2 + lax.axis_index("lat_2")
    return group * LATS


def window(j):
    return pl.multiple_of((j * 7 // 2) * 128, 128)


def lanes_as_bf16():
    return lax.broadcasted_iota(jnp.int32, (16, 128), 1).astype(F32).astype(BF16)


def map_slots(ids, inv_ref, row, base, first):
    lane = lanes_as_bf16()
    local = ids[pl.ds(row, 16), :] - first
    inside = (local >= 0) & (local < LATS)
    code = jnp.where(inside, local, 8 * 128)
    low = (code & 127).astype(F32).astype(BF16)
    high = (code >> 7).astype(F32).astype(BF16)
    for side in range(2):
        found = [jnp.full((16, 128), NONE, BF16) for _ in range(8)]
        for k in range(SLOTS):
            at = side * SLOTS + k
            here = lane == jnp.broadcast_to(low[:, at : at + 1], (16, 128))
            tile = jnp.where(
                here, jnp.broadcast_to(high[:, at : at + 1], (16, 128)), jnp.array(8, BF16)
            )
            slot = jnp.array(k, BF16)
            for c in range(8):
                found[c] = jnp.where(tile == jnp.array(c, BF16), slot, found[c])
        start = pl.multiple_of(base + side * 128 + row, 16)
        for c in range(8):
            inv_ref[pl.ds(start, 16), c * 128 : (c + 1) * 128] = found[c]


def opening_kernel(
    act_ref, dict_ref, ids_ref, lat_ref, inv_ref, ids8_ref,
    dbuf, dsem, id_send, id_recv, halo_send, halo_recv, own_sem,
):
    me = seat()
    seq = lax.axis_index("seq")
    for c in range(4):
        pltpu.make_async_copy(dict_ref.at[pl.ds(c * 256, 256)], dbuf.at[c], dsem.at[c]).start()
    enter(group_partners())
    sends = []
    for delta in range(1, GROUP):
        _, device = peer(delta)
        copy = remote(
            ids_ref, ids8_ref.at[me], id_send.at[delta - 1], id_recv.at[delta - 1], device
        )
        copy.start()
        sends.append(copy)
    own_ids = pltpu.make_async_copy(ids_ref, ids8_ref.at[me], own_sem)
    own_ids.start()

    def encode(c, carry):
        pltpu.make_async_copy(dict_ref.at[pl.ds(0, 256)], dbuf.at[c], dsem.at[c]).wait()
        lanes = pl.ds(pl.multiple_of(c * 256, 256), 256)
        lat_ref[8 : 8 + TOK, lanes] = lax.dot_general(
            act_ref[...], dbuf[c], (((1,), (1,)), ((), ())), preferred_element_type=F32
        )
        return carry

    lax.fori_loop(0, 4, encode, 0)
    left = {"seq": lax.rem(seq + 3, 4)}
    right = {"seq": lax.rem(seq + 1, 4)}
    to_left = remote(
        lat_ref.at[pl.ds(8, 8)], lat_ref.at[pl.ds(8 + TOK, 8)], halo_send.at[0], halo_recv.at[0], left
    )
    to_right = remote(
        lat_ref.at[pl.ds(TOK, 8)], lat_ref.at[pl.ds(0, 8)], halo_send.at[1], halo_recv.at[1], right
    )
    to_left.start()
    to_right.start()

    def own_slots(block, carry):
        map_slots(ids_ref, inv_ref, pl.multiple_of(block * 16, 16), 0, first_latent())
        return carry

    lax.fori_loop(0, 8, own_slots, 0)
    own_ids.wait()
    for delta in range(1, GROUP):
        pltpu.make_async_copy(ids_ref, ids8_ref.at[0], id_recv.at[delta - 1]).wait()
    to_left.wait()
    to_right.wait()
    lat_ref[0:8, :] = jnp.where(seq > 0, lat_ref[0:8, :], 0.0)
    lat_ref[8 + TOK :, :] = jnp.where(seq < 3, lat_ref[8 + TOK :, :], 0.0)
    for copy in sends:
        copy.wait_send()


def opening(act, dictionary, ids):
    return pl.pallas_call(
        opening_kernel,
        out_shape=(
            jax.ShapeDtypeStruct((TOK + 16, LATS), F32),
            jax.ShapeDtypeStruct((TOK, LATS), BF16),
            jax.ShapeDtypeStruct((GROUP, 128, 128), jnp.int32),
        ),
        in_specs=[VMEM, ANY, VMEM],
        out_specs=(VMEM, VMEM, VMEM),
        scratch_shapes=[
            pltpu.VMEM((4, 256, D), BF16),
            pltpu.SemaphoreType.DMA((4,)),
            pltpu.SemaphoreType.DMA((7,)),
            pltpu.SemaphoreType.DMA((7,)),
            pltpu.SemaphoreType.DMA((2,)),
            pltpu.SemaphoreType.DMA((2,)),
            pltpu.SemaphoreType.DMA,
        ],
        compiler_params=pltpu.CompilerParams(
            collective_id=0, has_side_effects=True, vmem_limit_bytes=32 * 1024 * 1024
        ),
        name="opening",
    )(act, dictionary, ids)


def sum_kernel(
    part_ref, act_ref, ids8_ref, own_inv_ref, res8_ref, cols_ref, inv_ref,
    half, down_out, down_in, up_out, up_in, own_sum, other_sum, res, slices,
    half_sem, dsend, drecv, usend, urecv, xsend, xrecv, asend, arecv,
    gdsend, gdrecv, gusend, gurecv, csend, crecv, act_send, act_recv, own_sem,
):
    me = seat()
    core = lax.axis_index("lat_2")
    z = lax.axis_index("lat_1")
    x = lax.axis_index("lat_0")
    first = first_latent()
    other_core = {"lat_2": 1 - core}
    below = {"lat_1": lax.rem(z + 7, 8)}
    above = {"lat_1": lax.rem(z + 1, 8)}
    other_x = {"lat_0": 1 - x}
    give = pl.multiple_of((1 - core) * 128, 128)
    keep = pl.multiple_of(core * 128, 128)
    rows = pl.multiple_of(keep + z * 16, 16)

    def work(n):
        j = lax.rem(me + 1 + n // 8, GROUP)
        row = pl.multiple_of(lax.rem(n, 8) * 16, 16)
        map_slots(ids8_ref.at[j], inv_ref, row, j * TOK, first)

    def work_many(begin, end):
        def step(n, carry):
            work(n)
            return carry

        lax.fori_loop(begin, end, step, 0)

    own_inv = pltpu.make_async_copy(
        own_inv_ref, inv_ref.at[pl.ds(pl.multiple_of(me * TOK, TOK), TOK)], own_sem.at[0]
    )
    own_inv.start()
    own_cols = pltpu.make_async_copy(
        act_ref.at[:, pl.ds(window(me), WIN)], cols_ref.at[me], own_sem.at[1]
    )
    own_cols.start()
    enter([other_core, below, above, other_x] + group_partners())

    def half_copy():
        return remote(
            part_ref.at[pl.ds(give, 128)], half, half_sem.at[0], half_sem.at[1], other_core
        )

    def act_copy(delta):
        j, device = peer(delta)
        return remote(
            act_ref.at[:, pl.ds(window(j), WIN)],
            cols_ref.at[me],
            act_send.at[delta - 1],
            act_recv.at[delta - 1],
            device,
        )

    half_copy().start()
    for delta in range(1, GROUP):
        act_copy(delta).start()
    work_many(0, 3)
    half_copy().wait_recv()
    width = D // PIECES

    def cols_of(h):
        return pl.ds(pl.multiple_of(h * width, width), width)

    def mine(chunk, h):
        at = pl.multiple_of(chunk * 16, 16)
        return part_ref[pl.ds(keep + at, 16), cols_of(h)].astype(F32) + half[
            pl.ds(at, 16), cols_of(h)
        ].astype(F32)

    def down_copy(s, h):
        return remote(
            down_out.at[s, :, cols_of(h)],
            down_in.at[s, :, cols_of(h)],
            dsend.at[s, h],
            drecv.at[s, h],
            below,
        )

    def up_copy(s, h):
        return remote(
            up_out.at[s, :, cols_of(h)],
            up_in.at[s, :, cols_of(h)],
            usend.at[s, h],
            urecv.at[s, h],
            above,
        )

    def x_copy(h):
        return remote(
            own_sum.at[:, cols_of(h)], other_sum.at[:, cols_of(h)], xsend.at[h], xrecv.at[h], other_x
        )

    def far_sums(h, carry):
        down_out[0, :, cols_of(h)] = mine(lax.rem(z + 4, 8), h).astype(BF16)
        down_copy(0, h).start()
        up_out[0, :, cols_of(h)] = mine(lax.rem(z + 3, 8), h).astype(BF16)
        up_copy(0, h).start()
        return carry

    lax.fori_loop(0, PIECES, far_sums, 0)

    def near_sums(i, carry):
        s, h = i // PIECES + 1, lax.rem(i, PIECES)
        work(3 + i)
        down_copy(s - 1, h).wait_recv()
        down_out[s, :, cols_of(h)] = (
            mine(lax.rem(z + 4 + s, 8), h) + down_in[s - 1, :, cols_of(h)].astype(F32)
        ).astype(BF16)
        down_copy(s, h).start()

        @pl.when(s <= 2)
        def _():
            up_copy(s - 1, h).wait_recv()
            up_out[s, :, cols_of(h)] = (
                mine(lax.rem(z + 3 - s, 8), h) + up_in[s - 1, :, cols_of(h)].astype(F32)
            ).astype(BF16)
            up_copy(s, h).start()

        return carry

    lax.fori_loop(0, 3 * PIECES, near_sums, 0)

    def last_sums(h, carry):
        work(15 + h)
        down_copy(3, h).wait_recv()
        up_copy(2, h).wait_recv()
        total = mine(z, h) + down_in[3, :, cols_of(h)].astype(F32)
        total = total + up_in[2, :, cols_of(h)].astype(F32)
        own_sum[:, cols_of(h)] = total.astype(BF16)
        x_copy(h).start()
        return carry

    lax.fori_loop(0, PIECES, last_sums, 0)
    work_many(19, 23)
    for h in range(PIECES):
        x_copy(h).wait_recv()
    res[...] = (own_sum[...].astype(F32) + other_sum[...].astype(F32)) - act_ref[
        pl.ds(rows, 16), :
    ].astype(F32)
    for j in range(GROUP):
        begin = (j * 7 // 2) * 128
        column = lax.broadcasted_iota(jnp.int32, (16, WIN), 1) + begin
        owned = (column >= j * OWN) & (column < (j + 1) * OWN)
        slices[j] = jnp.where(owned, res[:, begin : begin + WIN], 0.0).astype(BF16)

    def slice_copy(delta):
        j, device = peer(delta)
        return remote(
            slices.at[j],
            res8_ref.at[me, pl.ds(rows, 16)],
            asend.at[delta - 1],
            arecv.at[delta - 1],
            device,
        )

    for delta in range(1, GROUP):
        slice_copy(delta).start()
    own = pltpu.make_async_copy(slices.at[me], res8_ref.at[me, pl.ds(rows, 16)], own_sem.at[2])
    own.start()
    work_many(23, 28)
    own.wait()
    for delta in range(1, GROUP):
        slice_copy(delta).wait_recv()

    def region(chunk, h):
        at = pl.multiple_of(keep + chunk * 16, 16)
        return res8_ref.at[pl.ds(h * 2, 2), pl.ds(at, 16)]

    def chunk_rows(base, chunk):
        at = pl.multiple_of(base + chunk * 16, 16)
        return res8_ref.at[:, pl.ds(at, 16)]

    def down_region(s, h):
        chunk = region(lax.rem(z + s, 8), h)
        return remote(chunk, chunk, gdsend.at[s, h], gdrecv.at[s, h], below)

    def up_region(s, h):
        chunk = region(lax.rem(z + 8 - s, 8), h)
        return remote(chunk, chunk, gusend.at[s, h], gurecv.at[s, h], above)

    def arrived(sem, chunk, h):
        pltpu.make_async_copy(region(chunk, h), region(chunk, h), sem).wait()

    def core_copy(chunk, n):
        part = chunk_rows(keep, chunk)
        return remote(part, part, csend.at[n], crecv.at[n], other_core)

    def first_regions(h, carry):
        down_region(0, h).start()
        up_region(0, h).start()
        return carry

    lax.fori_loop(0, 4, first_regions, 0)
    core_copy(z, 0).start()

    def next_regions(i, carry):
        s, h = i // 4 + 1, lax.rem(i, 4)
        work(28 + i)
        arrived(gdrecv.at[s - 1, h], lax.rem(z + s, 8), h)
        down_region(s, h).start()
        arrived(gurecv.at[s - 1, h], lax.rem(z + 8 - s, 8), h)

        @pl.when(s <= 2)
        def _():
            up_region(s, h).start()

        @pl.when(h == 3)
        def _():
            core_copy(lax.rem(z + s, 8), s).start()
            core_copy(lax.rem(z + 8 - s, 8), s + 4).start()

        return carry

    lax.fori_loop(0, 12, next_regions, 0)
    work_many(40, 44)
    for h in range(4):
        arrived(gdrecv.at[3, h], lax.rem(z + 4, 8), h)
    core_copy(lax.rem(z + 4, 8), 4).start()
    work_many(44, 56)
    for n in range(8):
        chunk = lax.rem(z + n, 8) if n < 5 else lax.rem(z + 12 - n, 8)
        part = chunk_rows(give, chunk)
        pltpu.make_async_copy(part, part, crecv.at[n]).wait()
    own_inv.wait()
    own_cols.wait()
    for delta in range(1, GROUP):
        act_copy(delta).wait_recv()
        act_copy(delta).wait_send()
        slice_copy(delta).wait_send()
    half_copy().wait_send()
    for h in range(PIECES):
        x_copy(h).wait_send()
    for n in range(8):
        core_copy(z, n).wait_send()

    def sent(i, carry):
        s, h = i // 4, lax.rem(i, 4)
        down_copy(s, h).wait_send()
        down_region(s, h).wait_send()

        @pl.when(s <= 2)
        def _():
            up_copy(s, h).wait_send()
            up_region(s, h).wait_send()

        return carry

    lax.fori_loop(0, 16, sent, 0)


def summed(part, act, ids8, own_inv):
    dma = pltpu.SemaphoreType.DMA
    return pl.pallas_call(
        sum_kernel,
        out_shape=(
            jax.ShapeDtypeStruct((GROUP, TOK, WIN), BF16),
            jax.ShapeDtypeStruct((GROUP, TOK, WIN), BF16),
            jax.ShapeDtypeStruct((GROUP * TOK, LATS), BF16),
        ),
        in_specs=[VMEM] * 4,
        out_specs=[VMEM] * 3,
        scratch_shapes=[
            pltpu.VMEM((128, D), BF16),
            pltpu.VMEM((4, 16, D), BF16),
            pltpu.VMEM((4, 16, D), BF16),
            pltpu.VMEM((3, 16, D), BF16),
            pltpu.VMEM((3, 16, D), BF16),
            pltpu.VMEM((16, D), BF16),
            pltpu.VMEM((16, D), BF16),
            pltpu.VMEM((16, D), F32),
            pltpu.VMEM((GROUP, 16, WIN), BF16),
            dma((2,)),
            dma((4, PIECES)),
            dma((4, PIECES)),
            dma((3, PIECES)),
            dma((3, PIECES)),
            dma((PIECES,)),
            dma((PIECES,)),
            dma((7,)),
            dma((7,)),
            dma((4, 4)),
            dma((4, 4)),
            dma((3, 4)),
            dma((3, 4)),
            dma((8,)),
            dma((8,)),
            dma((7,)),
            dma((7,)),
            dma((3,)),
        ],
        compiler_params=pltpu.CompilerParams(
            collective_id=1, has_side_effects=True, vmem_limit_bytes=40 * 1024 * 1024
        ),
        name="summed",
    )(part, act, ids8, own_inv)


def slots_of(read, ids, first):
    def rows(row):
        local = ids[pl.ds(row, 8), :] - first
        inside = (local >= 0) & (local < LATS)
        code = jnp.where(inside, local, 8 * 128)
        low, high = code & 127, code >> 7
        second = lax.broadcasted_iota(jnp.int32, (8, 128), 1) >= SLOTS
        total = jnp.zeros((8, 128), F32)
        for c in range(8):
            one = jnp.take_along_axis(read(row, c), low, axis=1)
            two = jnp.take_along_axis(read(row + 128, c), low, axis=1)
            total = jnp.where(high == c, jnp.where(second, two, one), total)
        return total

    return rows


def pick_slots(value_ref, ids, into, first):
    def step(block, carry):
        for part in range(2):
            row = pl.multiple_of(block * 32 + part * 16, 16)
            halves = []
            for side in range(2):
                at = pl.multiple_of(row + side * 8, 8)
                rows = slots_of(
                    lambda r, c: value_ref[pl.ds(r, 8), c * 128 : (c + 1) * 128], ids, first
                )
                halves.append(rows(at))
            into[pl.ds(row, 16), :] = jnp.concatenate(halves, axis=0).astype(BF16)
        return carry

    lax.fori_loop(0, 4, step, 0)


def codes_kernel(
    latents_ref, res8_ref, dict_ref, ids8_ref, inv_ref, lat_ref,
    total_ref, codes8_ref, small_ref,
    dwin, dense, codes, part, arrived, own_total, small_part, small_in,
    psend, precv, csend, crecv, tsend, trecv, ssend, srecv, own_sem,
):
    me = seat()
    first = first_latent()
    dict_copy = pltpu.make_async_copy(
        dict_ref.at[:, pl.ds(window(me), WIN)], dwin, own_sem.at[0]
    )
    dict_copy.start()
    dense[...] = latents_ref[...].astype(F32)
    pick_slots(dense, ids8_ref.at[me], codes, first)
    enter(group_partners())

    def code_copy(delta):
        return remote(
            codes, codes8_ref.at[me], csend.at[delta - 1], crecv.at[delta - 1], peer(delta)[1]
        )

    def part_copy(delta):
        j, device = peer(delta)
        return remote(part.at[j], arrived.at[me], psend.at[delta - 1], precv.at[delta - 1], device)

    def total_copy(delta):
        return remote(
            own_total, total_ref.at[me], tsend.at[delta - 1], trecv.at[delta - 1], peer(delta)[1]
        )

    def small_copy(delta):
        return remote(
            small_part, small_in.at[me], ssend.at[delta - 1], srecv.at[delta - 1], peer(delta)[1]
        )

    for delta in range(1, GROUP):
        code_copy(delta).start()
    dict_copy.wait()

    def block(n, carry):
        j = lax.rem(me + n, GROUP)
        dense[...] = lax.dot_general(
            res8_ref[j], dwin[...], (((1,), (1,)), ((), ())), preferred_element_type=F32
        )
        pick_slots(dense, ids8_ref.at[j], part.at[j], first)

        @pl.when(n < GROUP)
        def _():
            part_copy(n).start()

        return carry

    lax.fori_loop(1, GROUP + 1, block, 0)
    for delta in range(1, GROUP):
        part_copy(delta).wait_recv()
    arrived[me] = part[me]
    total = arrived[0].astype(F32)
    for j in range(1, GROUP):
        total = total + arrived[j].astype(F32)
    own_total[...] = total.astype(BF16)
    for delta in range(1, GROUP):
        total_copy(delta).start()
    keep = lax.broadcasted_iota(jnp.int32, (8, 128), 1) < SLOTS

    def expand(step, carry):
        row = pl.multiple_of(step * 16, 16)
        both = own_total[pl.ds(row, 16), :].astype(F32)
        for side in range(2):
            values = pltpu.roll(both, SLOTS, 1) if side else both
            at = pl.multiple_of(row + side * 128, 16)
            for c in range(8):
                lanes = slice(c * 128, (c + 1) * 128)
                slot = inv_ref[pl.ds(at, 16), lanes].astype(F32).astype(jnp.int32)
                for r in (0, 8):
                    dense[pl.ds(at + r, 8), lanes] = jnp.take_along_axis(
                        jnp.where(keep, values[r : r + 8], 0.0), slot[r : r + 8], axis=1
                    )
        return carry

    lax.fori_loop(0, 8, expand, 0)
    small_part[...] = jnp.zeros((16, LATS), F32)

    def correlate(c, carry):
        lanes = pl.ds(pl.multiple_of(c * 128, 128), 128)
        own = dense[:, lanes]
        wide = lat_ref[:, lanes]
        for k in range(TAPS):
            small_part[k : k + 1, lanes] = jnp.sum(
                own * wide[k + HALF : k + HALF + TOK], axis=0, keepdims=True
            )
        small_part[TAPS : TAPS + 1, lanes] = jnp.sum(own, axis=0, keepdims=True)
        return carry

    lax.fori_loop(0, 8, correlate, 0)
    for delta in range(1, GROUP):
        small_copy(delta).start()
    own_copies = [
        pltpu.make_async_copy(own_total, total_ref.at[me], own_sem.at[1]),
        pltpu.make_async_copy(codes, codes8_ref.at[me], own_sem.at[2]),
    ]
    for copy in own_copies:
        copy.start()
    small_in[me] = small_part[...]
    for copy in own_copies:
        copy.wait()
    for delta in range(1, GROUP):
        code_copy(delta).wait_recv()
        total_copy(delta).wait_recv()
        small_copy(delta).wait_recv()
    small = small_in[0]
    for j in range(1, GROUP):
        small = small + small_in[j]
    small_ref[...] = small
    for delta in range(1, GROUP):
        code_copy(delta).wait_send()
        part_copy(delta).wait_send()
        total_copy(delta).wait_send()
        small_copy(delta).wait_send()


def all_codes(latents, res8, dictionary, ids8, own_inv, lat):
    shape = jax.ShapeDtypeStruct((GROUP, 128, 128), BF16)
    dma = pltpu.SemaphoreType.DMA
    return pl.pallas_call(
        codes_kernel,
        out_shape=(shape, shape, jax.ShapeDtypeStruct((16, LATS), F32)),
        in_specs=[VMEM, VMEM, ANY, VMEM, VMEM, VMEM],
        out_specs=(VMEM, VMEM, VMEM),
        scratch_shapes=[
            pltpu.VMEM((LATS, WIN), BF16),
            pltpu.VMEM((TOK, LATS), F32),
            pltpu.VMEM((128, 128), BF16),
            pltpu.VMEM((GROUP, 128, 128), BF16),
            pltpu.VMEM((GROUP, 128, 128), BF16),
            pltpu.VMEM((128, 128), BF16),
            pltpu.VMEM((16, LATS), F32),
            pltpu.VMEM((GROUP, 16, LATS), F32),
        ]
        + [dma((7,))] * 8
        + [dma((3,))],
        compiler_params=pltpu.CompilerParams(
            collective_id=2, has_side_effects=True, vmem_limit_bytes=32 * 1024 * 1024
        ),
        name="all_codes",
    )(latents, res8, dictionary, ids8, own_inv, lat)


SEQ_ROWS = 4 * TOK + 16
UNROLL = 4


def dictionary_kernel(
    where_ref, inv_ref, codes_ref, grad_ref, res_ref, act_ref, taps_ref,
    out_ref, dense, pre, grad_in, res_t, act_t, product,
):
    width = inv_ref.shape[1]
    tiles = width // 128
    for c in range(tiles):
        for b in range(2):
            pre[c, b, 0:8, :] = jnp.zeros((8, 128), F32)
            pre[c, b, 8 + 4 * TOK :, :] = jnp.zeros((8, 128), F32)

    @pl.when(pl.program_id(0) == 0)
    def _():
        for j in range(GROUP):
            res_t[:, j * TOK : (j + 1) * TOK] = res_ref[j].T
            act_t[:, j * TOK : (j + 1) * TOK] = act_ref[j].T

    keep = lax.broadcasted_iota(jnp.int32, (16, 128), 1) < SLOTS

    def expand(block):
        j = block // 8
        row = pl.multiple_of(lax.rem(block, 8) * 16, 16)
        codes = codes_ref[j, pl.ds(row, 16), :].astype(F32)
        grad = grad_ref[j, pl.ds(row, 16), :].astype(F32)
        for side in range(2):
            if side:
                codes = pltpu.roll(codes, SLOTS, 1)
                grad = pltpu.roll(grad, SLOTS, 1)
            codes_side = jnp.where(keep, codes, 0.0)
            grad_side = jnp.where(keep, grad, 0.0)
            start = pl.multiple_of(j * TOK + side * 128 + row, 16)
            into = pl.multiple_of(8 + (j // 2) * TOK + side * 128 + row, 8)
            for c in range(tiles):
                at = slice(c * 128, (c + 1) * 128)
                slot = inv_ref[pl.ds(start, 16), at].astype(F32).astype(jnp.int32)
                wide = [
                    jnp.take_along_axis(codes_side[r : r + 8], slot[r : r + 8], axis=1)
                    for r in (0, 8)
                ]
                dense[pl.ds(start, 16), at] = jnp.concatenate(wide, axis=0).astype(BF16)
                for r in (0, 8):
                    pre[c, lax.rem(j, 2), pl.ds(into + r, 8), :] = jnp.take_along_axis(
                        grad_side[r : r + 8], slot[r : r + 8], axis=1
                    )

    def expand_some(step, carry):
        for u in range(UNROLL):
            expand(step * UNROLL + u)
        return carry

    lax.fori_loop(0, 64 // UNROLL, expand_some, 0)

    def spread(block, carry):
        b, row = block // 16, lax.rem(block, 16) * 64
        j = (row // TOK) * 2 + b
        into = pl.multiple_of(j * TOK + lax.rem(row, TOK), 64)
        for c in range(tiles):
            at = slice(c * 128, (c + 1) * 128)
            total = jnp.zeros((64, 128), F32)
            for k in range(TAPS):
                total = total + taps_ref[k : k + 1, at] * pre[c, b, pl.ds(row + (8 + HALF - k), 64), :]
            grad_in[pl.ds(into, 64), at] = total.astype(BF16)
        return carry

    lax.fori_loop(0, 32, spread, 0)
    product[...] = jnp.dot(
        res_t[...], dense[...], preferred_element_type=F32
    ) + jnp.dot(act_t[...], grad_in[...], preferred_element_type=F32)
    out_ref[...] = product[pl.ds(pl.multiple_of(where_ref[0], 64), OWN), :]


def dictionary_gradient(where, inv, codes8, grad8, res8, cols, taps):
    width = 256
    return pl.pallas_call(
        dictionary_kernel,
        grid=(LATS // width,),
        out_shape=jax.ShapeDtypeStruct((OWN, LATS), F32),
        in_specs=[
            pl.BlockSpec(memory_space=pltpu.SMEM),
            pl.BlockSpec((GROUP * TOK, width), lambda i: (0, i)),
            pl.BlockSpec((GROUP, 128, 128), lambda i: (0, 0, 0)),
            pl.BlockSpec((GROUP, 128, 128), lambda i: (0, 0, 0)),
            pl.BlockSpec((GROUP, TOK, WIN), lambda i: (0, 0, 0)),
            pl.BlockSpec((GROUP, TOK, WIN), lambda i: (0, 0, 0)),
            pl.BlockSpec((TAPS, width), lambda i: (0, i)),
        ],
        out_specs=pl.BlockSpec((OWN, width), lambda i: (0, i)),
        scratch_shapes=[
            pltpu.VMEM((GROUP * TOK, width), BF16),
            pltpu.VMEM((width // 128, 2, SEQ_ROWS, 128), F32),
            pltpu.VMEM((GROUP * TOK, width), BF16),
            pltpu.VMEM((WIN, GROUP * TOK), BF16),
            pltpu.VMEM((WIN, GROUP * TOK), BF16),
            pltpu.VMEM((WIN, width), F32),
        ],
        name="dictionary_gradient",
    )(where, inv, codes8, grad8, res8, cols, taps)


def body(activations, dictionary, topk_ids, kernel_taps, enc_bias):
    act = activations[0]
    ids = topk_ids[0]
    ids = jnp.concatenate([ids[:128], ids[128:]], axis=1)
    lat, own_inv, ids8 = opening(act, dictionary, ids)
    preact = jnp.zeros((TOK, LATS), F32)
    for k in range(TAPS):
        preact = preact + kernel_taps[k][None, :] * lat[k + HALF : k + HALF + TOK]
    preact = preact + enc_bias[None, :]
    latents = jnp.where(own_inv < NONE, preact, 0.0).astype(BF16)
    part = jnp.einsum("tl,ld->td", latents, dictionary, preferred_element_type=F32).astype(BF16)
    res8, cols, inv = summed(part, act, ids8, own_inv)
    grad8, codes8, small = all_codes(latents, res8, dictionary, ids8, own_inv, lat)
    where = (lax.axis_index("batch") * 64).astype(jnp.int32)[None]
    gradient = dictionary_gradient(where, inv, codes8, grad8, res8, cols, kernel_taps)
    return gradient.T, small[:TAPS], small[TAPS]


def solution(mesh):
    finer = Mesh(
        mesh.devices.reshape(mesh.shape["seq"], 2, 8, 2, mesh.shape["batch"]),
        ("seq", "lat_0", "lat_1", "lat_2", "batch"),
    )
    return jax.shard_map(
        body,
        mesh=finer,
        in_specs=(
            P("batch", "seq", None),
            P(LAT, None),
            P("batch", "seq", None),
            P(None, LAT),
            P(LAT),
        ),
        out_specs=(P(LAT, ("seq", "batch")), P(None, LAT), P(LAT)),
        check_vma=False,
    )
```

time: 318 us -> 142 us (0.45)
  waiting for transfers between devices: 139 us -> 0 us
  Pallas kernels: 0 us -> 127 us
  blocking collectives: 77.1 us -> 0 us
  matrix products: 30.1 us -> 2.06 us
  starting transfers between devices: 19.8 us -> 0 us
  other arithmetic: 15.7 us -> 1.43 us
  between operations: 14.4 us -> 0.82 us
  local copies, waits for them, and re-layouts: 19.7 us -> 9.44 us
    pallas_call x0 -> x4, Pallas kernels: none -> 127 us  [the longest x1 61.5 us: summed(): pl.pallas_call(sum_kernel, out_shape=(jax.ShapeDtypeStruct((GROUP, TOK, W...]
    unnamed x2 -> x0, waiting for transfers between devices: 123 us -> none
    all_to_all x4 -> x0, blocking collectives: 77.1 us -> none  [the longest x1 36.7 us: summed_rows(): lax.all_to_all(nearer.astype(jnp.bfloat16), far, split_axis=0, concat_axi...]
    dot_general x5 -> x1, matrix products: 30.1 us -> 2.06 us  [body(): jnp.einsum('tl,ld->td', latents, dictionary, preferred_element_type=F32)]
    all_to_all x2 -> x0, waiting for transfers between devices: 15.9 us -> none  [copy_for_each(): lax.all_to_all(jnp.broadcast_to(shard[None], (devices, *shard.shape)), ax...]
    ppermute x4 -> x0, starting transfers between devices: 11.9 us -> none  [the longest x2 9.27 us: extended(): lax.ppermute(tail, axis, [(i, (i + 1) % count) for i in range(ends)])]
    unnamed x19 -> x25, local copies, waits for them, and re-layouts: 17.8 us -> 6.86 us
    reduce_or x1 -> x0, other arithmetic: 9.43 us -> none  [body(): jnp.any(chosen_ids[:, :, None] == latent_ids[None, None, :], axis=1)]
  transfers between devices with their start and end apart: 7 -> 0, of which waited for: 3 -> 0; matrix products, arithmetic and copies ran while one was open for 7% -> 0% of each run, Pallas kernels for 0% -> 0%
where the time goes in v2:
time: 142 us; the launch traced here: 141 us
  Pallas kernels  127 us (89%)
  local copies, waits for them, and re-layouts  9.44 us (7%)
  matrix products  2.06 us (1%)
  other arithmetic  1.43 us (1%)
    pallas_call x1, Pallas kernels, summed(): pl.pallas_call(sum_kernel, out_shape=(jax.ShapeDtypeStruct((GROUP, TOK, W...  61.5 us
    pallas_call x1, Pallas kernels, dictionary_gradient(): pl.pallas_call(dictionary_kernel, grid=(LATS // width,), out_shape=jax.Sh...  30 us
    pallas_call x1, Pallas kernels, all_codes(): pl.pallas_call(codes_kernel, out_shape=(shape, shape, jax.ShapeDtypeStruc...  23 us
    pallas_call x1, Pallas kernels, opening(): pl.pallas_call(opening_kernel, out_shape=(jax.ShapeDtypeStruct((TOK + 16,...  12.7 us
    unnamed x25, local copies, waits for them, and re-layouts  6.86 us

profile of v2, /device:TPU:32, one launch (start us, length us, event | category | flops | bytes accessed | tf_op | source)
XLA Modules:
  0.0 141.0 jit_solution(2121909794500958668)
XLA Ops:
  0.6 1.2 fusion
  1.8 0.8 fusion.1
  2.6 0.1 copy.10
  2.7 0.1 copy.11
  2.8 0.1 pad_add_fusion.ids_ref
  2.9 0.0 copy-start
  2.9 3.1 %copy-done = bf16[1024,3584]{1,0:T(8,128)(2,1)S(1)} copy-done((bf16[1024,3584]{1,0:T(8,128)(2,1)S(1)}, bf16[1024,3584]{1,0:T(8,128)(2,1)}, u32[]{:S(2)}) %copy-start) | copy-done | bytes 7340056
  6.0 1.5 %copy-done.2 = bf16[1,256,3584]{2,1,0:T(8,128)(2,1)S(1)} copy-done((bf16[1,256,3584]{2,1,0:T(8,128)(2,1)S(1)}, bf16[1,256,3584]{2,1,0:T(8,128)(2,1)}, u32[]{:S(2)}) %copy-start.2) | copy-done | bytes 1835032
  7.5 12.7 %opening.1 = (f32[272,1024]{1,0:T(8,128)S(1)}, bf16[256,1024]{1,0:T(8,128)(2,1)S(1)}, s32[8,128,128]{2,1,0:T(8,128)S(1)}) custom-call(bf16[256,3584]{1,0:T(8,128)(2,1)S(1)} %bitcast.20, bf16[1024,3584]{1,0:T(8,128)(2,1)S(1)} %copy-done, s32[128,128]{1,0:T(8,128)S(1)} %pad_add_fusion.ids_ref), custom_call_target="tpu_custom_call" | custom-call | tf_op jit(solution)/shard_map/opening/pallas_call | solution.py:159
  20.2 0.0 copy-done.8
  20.2 0.0 slice-start
  20.2 1.3 select_convert_fusion.latents_ref
  21.6 0.0 copy-start.3
  21.6 0.0 slice-start.1
  21.6 2.1 %convolution_convert_fusion.part_ref = bf16[256,3584]{1,0:T(8,128)(2,1)S(1)} fusion(bf16[256,1024]{1,0:T(8,128)(2,1)S(1)} %select_convert_fusion.latents_ref, bf16[1024,3584]{1,0:T(8,128)(2,1)S(1)} %copy-done), kind=kOutput, calls=%fused_computation | convolution fusion | flops 1879965696 | bytes 9699328 | tf_op jit(solution)/shard_map/tl,ld->td/dot_general | solution.py:778
  23.7 0.0 copy-done.3
  23.7 61.5 %summed.1 = (bf16[8,256,512]{2,1,0:T(8,128)(2,1)S(1)}, bf16[8,256,512]{2,1,0:T(8,128)(2,1)S(1)}, bf16[2048,1024]{1,0:T(8,128)(2,1)S(1)}) custom-call(bf16[256,3584]{1,0:T(8,128)(2,1)S(1)} %convolution_convert_fusion.part_ref, bf16[256,3584]{1,0:T(8,128)(2,1)S(1)} %bitcast.21, s32[8,128,128]{2,1,0:T(8,128)S(1)} %get-tuple-element.14.ids8_ref, ...), custom_call_target="tpu_custom_call" | custom-call | tf_op jit(solution)/shard_map/summed/pallas_call | solution.py:439
  85.2 0.0 copy-start.1
  85.2 0.0 copy-start.4
  85.2 0.0 copy-start.5
  85.2 0.0 slice-done
  85.2 0.0 slice-done.1
  85.2 23.0 %all_codes.1 = (bf16[8,128,128]{2,1,0:T(8,128)(2,1)S(1)}, bf16[8,128,128]{2,1,0:T(8,128)(2,1)S(1)}, f32[16,1024]{1,0:T(8,128)S(1)}) custom-call(bf16[256,1024]{1,0:T(8,128)(2,1)S(1)} %select_convert_fusion.latents_ref, bf16[8,256,512]{2,1,0:T(8,128)(2,1)S(1)} %get-tuple-element.16.res8_ref.res_ref, bf16[1024,3584]{1,0:T(8,128)(2,1)S(1)} %bitcast.19, ...), custom_call_target="tpu_custom_call" | custom-call | tf_op jit(solution)/shard_map/all_codes/pallas_call | solution.py:641
  108.3 0.0 copy-done.1
  108.3 0.0 copy-done.4
  108.3 0.0 copy-done.5
  108.3 0.0 copy-start.6
  108.3 0.7 copy-done.6
  109.0 0.7 copy-done.7
  109.7 30.0 %dictionary_gradient.1 = f32[448,1024]{1,0:T(8,128)} custom-call(s32[1]{0:T(128)} %bitcast.where_ref, bf16[2048,1024]{1,0:T(8,128)(2,1)} %copy-done.4, bf16[8,128,128]{2,1,0:T(8,128)(2,1)} %copy-done.7, bf16[8,128,128]{2,1,0:T(8,128)(2,1)} %copy-done.6, bf16[8,256,512]{2,1,0:T(8,128)(2,1)} %copy-done.1, bf16[8,256,512]{2,1,0:T(8,128)(2,1)} %copy-done.5, ...), custom_call_target="tpu_custom_call" | custom-call | tf_op jit(solution)/shard_map/dictionary_gradient/pallas_call | solution.py:742
  139.7 0.6 slice.95
  140.3 0.6 copy.13
  (4 shorter events, 0.0 us)
Async XLA Ops:
  2.9 3.1 %copy-start = (bf16[1024,3584]{1,0:T(8,128)(2,1)S(1)}, bf16[1024,3584]{1,0:T(8,128)(2,1)}, u32[]{:S(2)}) copy-start(bf16[1024,3584]{1,0:T(8,128)(2,1)} %dict_ref.3) | copy-start | bytes 22020100
  6.0 1.5 %copy-start.2 = (bf16[1,256,3584]{2,1,0:T(8,128)(2,1)S(1)}, bf16[1,256,3584]{2,1,0:T(8,128)(2,1)}, u32[]{:S(2)}) copy-start(bf16[1,256,3584]{2,1,0:T(8,128)(2,1)} %param.5) | copy-start | bytes 5505028
  7.5 12.7 %copy-start.8 = (f32[1024]{0:T(1024)S(1)}, f32[1024]{0:T(1024)}, u32[]{:S(2)}) copy-start(f32[1024]{0:T(1024)} %param.9) | copy-start | bytes 12292
  20.2 65.0 %slice-start = ((s8[7340032]{0:T(1024)(128)(4,1)}), s8[4194304]{0:T(1024)(128)(4,1)S(1)}, s32[]{:S(2)}) async-start(s8[7340032]{0:T(1024)(128)(4,1)} %bitcast.18), calls=%async_computation | async-start | bytes 8388608
  21.6 2.1 %copy-start.3 = (bf16[1,256,3584]{2,1,0:T(8,128)(2,1)S(1)}, bf16[1,256,3584]{2,1,0:T(8,128)(2,1)}, u32[]{:S(2)}) copy-start(bf16[1,256,3584]{2,1,0:T(8,128)(2,1)} %param.5) | copy-start | bytes 5505028
  21.6 63.6 %slice-start.1 = ((s8[7340032]{0:T(1024)(128)(4,1)}), s8[3145728]{0:T(1024)(128)(4,1)S(1)}, s32[]{:S(2)}) async-start(s8[7340032]{0:T(1024)(128)(4,1)} %bitcast.18), calls=%async_computation.1 | async-start | bytes 6291456
  85.2 23.1 %copy-start.1 = (bf16[8,256,512]{2,1,0:T(8,128)(2,1)}, bf16[8,256,512]{2,1,0:T(8,128)(2,1)S(1)}, u32[]{:S(2)}) copy-start(bf16[8,256,512]{2,1,0:T(8,128)(2,1)S(1)} %get-tuple-element.16.res8_ref.res_ref) | copy-start | bytes 6291460
  85.2 23.1 %copy-start.4 = (bf16[2048,1024]{1,0:T(8,128)(2,1)}, bf16[2048,1024]{1,0:T(8,128)(2,1)S(1)}, u32[]{:S(2)}) copy-start(bf16[2048,1024]{1,0:T(8,128)(2,1)S(1)} %get-tuple-element.15.inv_ref) | copy-start | bytes 12582916
  85.2 23.1 %copy-start.5 = (bf16[8,256,512]{2,1,0:T(8,128)(2,1)}, bf16[8,256,512]{2,1,0:T(8,128)(2,1)S(1)}, u32[]{:S(2)}) copy-start(bf16[8,256,512]{2,1,0:T(8,128)(2,1)S(1)} %get-tuple-element.19.act_ref) | copy-start | bytes 6291460
  108.3 0.7 copy-start.6
  109.0 0.7 copy-start.7

commit v3 on v2

--- a/solution.py
+++ b/solution.py
@@ -18,14 +18,13 @@
 OWN = 448
 WIN = 512
 GROUP = 8
-NONE = 64
 PIECES = 4
 F32 = jnp.float32
 BF16 = jnp.bfloat16
 MESH = pl.DeviceIdType.MESH
 VMEM = pl.BlockSpec(memory_space=pltpu.VMEM)
 ANY = pl.BlockSpec(memory_space=pl.ANY)
-BIG = 64 * 1024 * 1024 - 65536
+OPENING_MIB = 50
 
 
 def seat():
@@ -72,42 +71,79 @@
     return pl.multiple_of((j * 7 // 2) * 128, 128)
 
 
-def lanes_as_bf16():
-    return lax.broadcasted_iota(jnp.int32, (16, 128), 1).astype(F32).astype(BF16)
-
-
-def map_slots(ids, inv_ref, row, base, first):
-    lane = lanes_as_bf16()
-    local = ids[pl.ds(row, 16), :] - first
-    inside = (local >= 0) & (local < LATS)
-    code = jnp.where(inside, local, 8 * 128)
-    low = (code & 127).astype(F32).astype(BF16)
-    high = (code >> 7).astype(F32).astype(BF16)
-    for side in range(2):
-        found = [jnp.full((16, 128), NONE, BF16) for _ in range(8)]
-        for k in range(SLOTS):
-            at = side * SLOTS + k
-            here = lane == jnp.broadcast_to(low[:, at : at + 1], (16, 128))
-            tile = jnp.where(
-                here, jnp.broadcast_to(high[:, at : at + 1], (16, 128)), jnp.array(8, BF16)
-            )
-            slot = jnp.array(k, BF16)
-            for c in range(8):
-                found[c] = jnp.where(tile == jnp.array(c, BF16), slot, found[c])
-        start = pl.multiple_of(base + side * 128 + row, 16)
-        for c in range(8):
-            inv_ref[pl.ds(start, 16), c * 128 : (c + 1) * 128] = found[c]
+def slot_rows(ids, side, first, rows_ref):
+    code = ids[:, pl.ds(pl.multiple_of(side * 128, 128), 128)] - first
+    inside = (code >= 0) & (code < LATS)
+    hi = code >> 7
+    part = hi & 3
+    scale = jnp.where(
+        part == 0, 1, jnp.where(part == 1, 1 << 7, jnp.where(part == 2, 1 << 14, 1 << 21))
+    )
+    value = (lax.broadcasted_iota(jnp.int32, (SLOTS, 128), 0) + SLOTS) * scale
+    rows_ref[0] = jnp.where(inside, code & 127, -1)
+    rows_ref[1] = jnp.where(inside & (hi < 4), value, 0)
+    rows_ref[2] = jnp.where(inside & (hi >= 4), value, 0)
+
+
+def slot_half(side, half, inv_ref, base, rows_ref, found_ref):
+    sublane = lax.broadcasted_iota(jnp.int32, (8, 128), 0) + half * 64
+    found = [[jnp.zeros((8, 128), jnp.int32) for _ in range(2)] for _ in range(8)]
+    for k in range(SLOTS):
+        low = jnp.broadcast_to(rows_ref[0, k : k + 1, :], (8, 128))
+        values = [jnp.broadcast_to(rows_ref[1 + i, k : k + 1, :], (8, 128)) for i in range(2)]
+        for r in range(8):
+            here = low == sublane + r * 8
+            for i in range(2):
+                found[r][i] = found[r][i] + jnp.where(here, values[i], 0)
+    for r in range(8):
+        for i in range(2):
+            found_ref[i, r * 8 : (r + 1) * 8, :] = found[r][i]
+    into = pl.ds(pl.multiple_of(base + side * 128, 128), 128)
+    for i in range(2):
+        found_half = found_ref[i].T
+
+        @pl.when(half == 0)
+        def _():
+            inv_ref[into, i * 128 : i * 128 + 64] = found_half
+
+        @pl.when(half == 1)
+        def _():
+            inv_ref[into, i * 128 + 64 : (i + 1) * 128] = found_half
+
+
+def map_slots(n, ids, inv_ref, base, first, rows_ref, found_ref):
+    side, half = n // 2, lax.rem(n, 2)
+
+    @pl.when(half == 0)
+    def _():
+        slot_rows(ids, side, first, rows_ref)
+
+    slot_half(side, half, inv_ref, base, rows_ref, found_ref)
+
+
+def slot_lane(packed, shift):
+    return ((packed >> shift) + SLOTS) & 127
 
 
 def opening_kernel(
-    act_ref, dict_ref, ids_ref, lat_ref, inv_ref, ids8_ref,
-    dbuf, dsem, id_send, id_recv, halo_send, halo_recv, own_sem,
+    act_hbm, dict_ref, ids_hbm, taps_hbm, bias_hbm,
+    latents_ref, part_ref, dwin_ref, lat_ref, inv_ref, ids8_ref,
+    act_ref, dbuf, ids_ref, taps_ref, bias_ref, rows_ref, found_ref, dsem, id_send, id_recv, halo_send, halo_recv, own_sem,
 ):
     me = seat()
     seq = lax.axis_index("seq")
+    ids_copy = pltpu.make_async_copy(ids_hbm, ids_ref, own_sem.at[2])
+    act_copy = pltpu.make_async_copy(act_hbm, act_ref, own_sem.at[1])
+    taps_copy = pltpu.make_async_copy(taps_hbm, taps_ref, own_sem.at[3])
+    bias_copy = pltpu.make_async_copy(bias_hbm, bias_ref, own_sem.at[4])
+    for copy in (ids_copy, act_copy):
+        copy.start()
     for c in range(4):
         pltpu.make_async_copy(dict_ref.at[pl.ds(c * 256, 256)], dbuf.at[c], dsem.at[c]).start()
+    for copy in (taps_copy, bias_copy):
+        copy.start()
     enter(group_partners())
+    ids_copy.wait()
     sends = []
     for delta in range(1, GROUP):
         _, device = peer(delta)
@@ -116,76 +152,112 @@
         )
         copy.start()
         sends.append(copy)
-    own_ids = pltpu.make_async_copy(ids_ref, ids8_ref.at[me], own_sem)
+    own_ids = pltpu.make_async_copy(ids_ref, ids8_ref.at[me], own_sem.at[0])
     own_ids.start()
+    act_copy.wait()
 
     def encode(c, carry):
         pltpu.make_async_copy(dict_ref.at[pl.ds(0, 256)], dbuf.at[c], dsem.at[c]).wait()
-        lanes = pl.ds(pl.multiple_of(c * 256, 256), 256)
-        lat_ref[8 : 8 + TOK, lanes] = lax.dot_general(
+        both = lax.dot_general(
             act_ref[...], dbuf[c], (((1,), (1,)), ((), ())), preferred_element_type=F32
         )
+        lat_ref[2 * c, 8 : 8 + TOK, :] = both[:, :128]
+        lat_ref[2 * c + 1, 8 : 8 + TOK, :] = both[:, 128:]
         return carry
 
     lax.fori_loop(0, 4, encode, 0)
     left = {"seq": lax.rem(seq + 3, 4)}
     right = {"seq": lax.rem(seq + 1, 4)}
     to_left = remote(
-        lat_ref.at[pl.ds(8, 8)], lat_ref.at[pl.ds(8 + TOK, 8)], halo_send.at[0], halo_recv.at[0], left
+        lat_ref.at[:, pl.ds(8, 8)], lat_ref.at[:, pl.ds(8 + TOK, 8)],
+        halo_send.at[0], halo_recv.at[0], left,
     )
     to_right = remote(
-        lat_ref.at[pl.ds(TOK, 8)], lat_ref.at[pl.ds(0, 8)], halo_send.at[1], halo_recv.at[1], right
+        lat_ref.at[:, pl.ds(TOK, 8)], lat_ref.at[:, pl.ds(0, 8)],
+        halo_send.at[1], halo_recv.at[1], right,
     )
     to_left.start()
     to_right.start()
-
-    def own_slots(block, carry):
-        map_slots(ids_ref, inv_ref, pl.multiple_of(block * 16, 16), 0, first_latent())
-        return carry
-
-    lax.fori_loop(0, 8, own_slots, 0)
-    own_ids.wait()
-    for delta in range(1, GROUP):
-        pltpu.make_async_copy(ids_ref, ids8_ref.at[0], id_recv.at[delta - 1]).wait()
+    dwin_ref[...] = dbuf[:, :, pl.ds(window(me), WIN)].reshape(LATS, WIN)
+
+    def own_slots(n, carry):
+        map_slots(n, ids_ref, inv_ref, 0, first_latent(), rows_ref, found_ref)
+        return carry
+
+    lax.fori_loop(0, 4, own_slots, 0)
+    taps_copy.wait()
+    bias_copy.wait()
     to_left.wait()
     to_right.wait()
-    lat_ref[0:8, :] = jnp.where(seq > 0, lat_ref[0:8, :], 0.0)
-    lat_ref[8 + TOK :, :] = jnp.where(seq < 3, lat_ref[8 + TOK :, :], 0.0)
+    lat_ref[:, 0:8, :] = jnp.where(seq > 0, lat_ref[:, 0:8, :], 0.0)
+    lat_ref[:, 8 + TOK :, :] = jnp.where(seq < 3, lat_ref[:, 8 + TOK :, :], 0.0)
+    for c in range(8):
+        at = slice(c * 128, (c + 1) * 128)
+        total = jnp.zeros((TOK, 128), F32)
+        for k in range(TAPS):
+            total = total + taps_ref[k : k + 1, at] * lat_ref[c, k + HALF : k + HALF + TOK, :]
+        total = total + bias_ref[:, at]
+        packed = inv_ref[:, (c // 4) * 128 : (c // 4 + 1) * 128]
+        active = ((packed >> (7 * (c % 4))) & 127) != 0
+        latents_ref[:, at] = jnp.where(active, total, 0.0).astype(BF16)
+
+    def decode(n, carry):
+        at = pl.ds(pl.multiple_of(n * 512, 512), 512)
+        part_ref[:, at] = jnp.dot(
+            latents_ref[...], dbuf[:, :, at].reshape(LATS, 512), preferred_element_type=F32
+        ).astype(BF16)
+        return carry
+
+    lax.fori_loop(0, D // 512, decode, 0)
+    own_ids.wait()
+    for delta in range(1, GROUP):
+        pltpu.make_async_copy(ids_ref, ids8_ref.at[0], id_recv.at[delta - 1]).wait()
     for copy in sends:
         copy.wait_send()
 
 
-def opening(act, dictionary, ids):
+SLOT_SCRATCH = [pltpu.VMEM((3, SLOTS, 128), jnp.int32), pltpu.VMEM((2, 64, 128), jnp.int32)]
+
+
+def opening(act, dictionary, ids, taps, bias):
     return pl.pallas_call(
         opening_kernel,
         out_shape=(
-            jax.ShapeDtypeStruct((TOK + 16, LATS), F32),
             jax.ShapeDtypeStruct((TOK, LATS), BF16),
-            jax.ShapeDtypeStruct((GROUP, 128, 128), jnp.int32),
+            jax.ShapeDtypeStruct((TOK, D), BF16),
+            jax.ShapeDtypeStruct((LATS, WIN), BF16),
+            jax.ShapeDtypeStruct((8, TOK + 16, 128), F32),
+            jax.ShapeDtypeStruct((TOK, 256), jnp.int32),
+            jax.ShapeDtypeStruct((GROUP, SLOTS, TOK), jnp.int32),
         ),
-        in_specs=[VMEM, ANY, VMEM],
-        out_specs=(VMEM, VMEM, VMEM),
+        in_specs=[ANY] * 5,
+        out_specs=[VMEM] * 6,
         scratch_shapes=[
+            pltpu.VMEM((TOK, D), BF16),
             pltpu.VMEM((4, 256, D), BF16),
+            pltpu.VMEM((SLOTS, TOK), jnp.int32),
+            pltpu.VMEM((TAPS, LATS), F32),
+            pltpu.VMEM((1, LATS), F32),
+            *SLOT_SCRATCH,
             pltpu.SemaphoreType.DMA((4,)),
             pltpu.SemaphoreType.DMA((7,)),
             pltpu.SemaphoreType.DMA((7,)),
             pltpu.SemaphoreType.DMA((2,)),
             pltpu.SemaphoreType.DMA((2,)),
-            pltpu.SemaphoreType.DMA,
+            pltpu.SemaphoreType.DMA((5,)),
         ],
         compiler_params=pltpu.CompilerParams(
-            collective_id=0, has_side_effects=True, vmem_limit_bytes=32 * 1024 * 1024
+            collective_id=0, has_side_effects=True, vmem_limit_bytes=OPENING_MIB * 1024 * 1024
         ),
         name="opening",
-    )(act, dictionary, ids)
+    )(act, dictionary, ids, taps, bias)
 
 
 def sum_kernel(
-    part_ref, act_ref, ids8_ref, own_inv_ref, res8_ref, cols_ref, inv_ref,
-    half, down_out, down_in, up_out, up_in, own_sum, other_sum, res, slices,
+    part_ref, act_ref, ids8_ref, own_inv_ref, res8_ref, act_t_ref, inv_ref,
+    cols_ref, rows_ref, found_ref, half, down_out, down_in, up_out, up_in, own_sum, other_sum, res, slices,
     half_sem, dsend, drecv, usend, urecv, xsend, xrecv, asend, arecv,
-    gdsend, gdrecv, gusend, gurecv, csend, crecv, act_send, act_recv, own_sem,
+    gdsend, gdrecv, gusend, gurecv, csend, crecv, act_send, act_recv, swap_send, swap_recv, own_sem,
 ):
     me = seat()
     core = lax.axis_index("lat_2")
@@ -201,9 +273,10 @@
     rows = pl.multiple_of(keep + z * 16, 16)
 
     def work(n):
-        j = lax.rem(me + 1 + n // 8, GROUP)
-        row = pl.multiple_of(lax.rem(n, 8) * 16, 16)
-        map_slots(ids8_ref.at[j], inv_ref, row, j * TOK, first)
+        j = lax.rem(me + 1 + n // 4, GROUP)
+        map_slots(
+            lax.rem(n, 4), ids8_ref.at[j], inv_ref, j * TOK, first, rows_ref, found_ref
+        )
 
     def work_many(begin, end):
         def step(n, carry):
@@ -230,11 +303,17 @@
     def act_copy(delta):
         j, device = peer(delta)
         return remote(
-            act_ref.at[:, pl.ds(window(j), WIN)],
-            cols_ref.at[me],
+            act_ref.at[pl.ds(keep, 128), pl.ds(window(j), WIN)],
+            cols_ref.at[me, pl.ds(keep, 128)],
             act_send.at[delta - 1],
             act_recv.at[delta - 1],
             device,
+        )
+
+    def swap_copy(delta):
+        rows_here = cols_ref.at[peer_from(delta), pl.ds(keep, 128)]
+        return remote(
+            rows_here, rows_here, swap_send.at[delta - 1], swap_recv.at[delta - 1], other_core
         )
 
     half_copy().start()
@@ -307,7 +386,6 @@
     lax.fori_loop(0, 3 * PIECES, near_sums, 0)
 
     def last_sums(h, carry):
-        work(15 + h)
         down_copy(3, h).wait_recv()
         up_copy(2, h).wait_recv()
         total = mine(z, h) + down_in[3, :, cols_of(h)].astype(F32)
@@ -317,7 +395,7 @@
         return carry
 
     lax.fori_loop(0, PIECES, last_sums, 0)
-    work_many(19, 23)
+    work_many(15, 20)
     for h in range(PIECES):
         x_copy(h).wait_recv()
     res[...] = (own_sum[...].astype(F32) + other_sum[...].astype(F32)) - act_ref[
@@ -343,7 +421,10 @@
         slice_copy(delta).start()
     own = pltpu.make_async_copy(slices.at[me], res8_ref.at[me, pl.ds(rows, 16)], own_sem.at[2])
     own.start()
-    work_many(23, 28)
+    work_many(20, 24)
+    for delta in range(1, GROUP):
+        act_copy(delta).wait_recv()
+        swap_copy(delta).start()
     own.wait()
     for delta in range(1, GROUP):
         slice_copy(delta).wait_recv()
@@ -381,7 +462,24 @@
 
     def next_regions(i, carry):
         s, h = i // 4 + 1, lax.rem(i, 4)
-        work(28 + i)
+
+        @pl.when(i < 4)
+        def _():
+            work(24 + i)
+
+        @pl.when(i == 4)
+        def _():
+            own_cols.wait()
+
+        @pl.when(i > 4)
+        def _():
+            swap_copy(i - 4).wait_recv()
+
+        @pl.when(i >= 4)
+        def _():
+            j = lax.rem(me + 12 - i, GROUP)
+            act_t_ref[:, pl.ds(pl.multiple_of(j * TOK, TOK), TOK)] = cols_ref[j].T
+
         arrived(gdrecv.at[s - 1, h], lax.rem(z + s, 8), h)
         down_region(s, h).start()
         arrived(gurecv.at[s - 1, h], lax.rem(z + 8 - s, 8), h)
@@ -398,20 +496,17 @@
         return carry
 
     lax.fori_loop(0, 12, next_regions, 0)
-    work_many(40, 44)
     for h in range(4):
         arrived(gdrecv.at[3, h], lax.rem(z + 4, 8), h)
     core_copy(lax.rem(z + 4, 8), 4).start()
-    work_many(44, 56)
     for n in range(8):
         chunk = lax.rem(z + n, 8) if n < 5 else lax.rem(z + 12 - n, 8)
         part = chunk_rows(give, chunk)
         pltpu.make_async_copy(part, part, crecv.at[n]).wait()
     own_inv.wait()
-    own_cols.wait()
-    for delta in range(1, GROUP):
-        act_copy(delta).wait_recv()
+    for delta in range(1, GROUP):
         act_copy(delta).wait_send()
+        swap_copy(delta).wait_send()
         slice_copy(delta).wait_send()
     half_copy().wait_send()
     for h in range(PIECES):
@@ -440,12 +535,14 @@
         sum_kernel,
         out_shape=(
             jax.ShapeDtypeStruct((GROUP, TOK, WIN), BF16),
-            jax.ShapeDtypeStruct((GROUP, TOK, WIN), BF16),
-            jax.ShapeDtypeStruct((GROUP * TOK, LATS), BF16),
+            jax.ShapeDtypeStruct((WIN, GROUP * TOK), BF16),
+            jax.ShapeDtypeStruct((GROUP * TOK, 256), jnp.int32),
         ),
         in_specs=[VMEM] * 4,
         out_specs=[VMEM] * 3,
         scratch_shapes=[
+            pltpu.VMEM((GROUP, TOK, WIN), BF16),
+            *SLOT_SCRATCH,
             pltpu.VMEM((128, D), BF16),
             pltpu.VMEM((4, 16, D), BF16),
             pltpu.VMEM((4, 16, D), BF16),
@@ -472,10 +569,12 @@
             dma((8,)),
             dma((7,)),
             dma((7,)),
+            dma((7,)),
+            dma((7,)),
             dma((3,)),
         ],
         compiler_params=pltpu.CompilerParams(
-            collective_id=1, has_side_effects=True, vmem_limit_bytes=40 * 1024 * 1024
+            collective_id=1, has_side_effects=True, vmem_limit_bytes=24 * 1024 * 1024
         ),
         name="summed",
     )(part, act, ids8, own_inv)
@@ -516,19 +615,21 @@
 
 
 def codes_kernel(
-    latents_ref, res8_ref, dict_ref, ids8_ref, inv_ref, lat_ref,
+    latents_ref, res8_ref, dwin, ids8_ref, inv_ref, lat_ref,
     total_ref, codes8_ref, small_ref,
-    dwin, dense, codes, part, arrived, own_total, small_part, small_in,
+    dense, ids_rows, codes, part, arrived, own_total, small_part, small_out, small_in,
     psend, precv, csend, crecv, tsend, trecv, ssend, srecv, own_sem,
 ):
     me = seat()
     first = first_latent()
-    dict_copy = pltpu.make_async_copy(
-        dict_ref.at[:, pl.ds(window(me), WIN)], dwin, own_sem.at[0]
-    )
-    dict_copy.start()
     dense[...] = latents_ref[...].astype(F32)
-    pick_slots(dense, ids8_ref.at[me], codes, first)
+
+    def rows_of(j):
+        ids = ids8_ref[j]
+        ids_rows[...] = jnp.concatenate([ids[:, :128], ids[:, 128:]], axis=0).T
+
+    rows_of(me)
+    pick_slots(dense, ids_rows, codes, first)
     enter(group_partners())
 
     def code_copy(delta):
@@ -547,19 +648,19 @@
 
     def small_copy(delta):
         return remote(
-            small_part, small_in.at[me], ssend.at[delta - 1], srecv.at[delta - 1], peer(delta)[1]
+            small_out, small_in.at[me], ssend.at[delta - 1], srecv.at[delta - 1], peer(delta)[1]
         )
 
     for delta in range(1, GROUP):
         code_copy(delta).start()
-    dict_copy.wait()
 
     def block(n, carry):
         j = lax.rem(me + n, GROUP)
         dense[...] = lax.dot_general(
             res8_ref[j], dwin[...], (((1,), (1,)), ((), ())), preferred_element_type=F32
         )
-        pick_slots(dense, ids8_ref.at[j], part.at[j], first)
+        rows_of(j)
+        pick_slots(dense, ids_rows, part.at[j], first)
 
         @pl.when(n < GROUP)
         def _():
@@ -587,7 +688,8 @@
             at = pl.multiple_of(row + side * 128, 16)
             for c in range(8):
                 lanes = slice(c * 128, (c + 1) * 128)
-                slot = inv_ref[pl.ds(at, 16), lanes].astype(F32).astype(jnp.int32)
+                packed = inv_ref[pl.ds(at, 16), (c // 4) * 128 : (c // 4 + 1) * 128]
+                slot = slot_lane(packed, 7 * (c % 4))
                 for r in (0, 8):
                     dense[pl.ds(at + r, 8), lanes] = jnp.take_along_axis(
                         jnp.where(keep, values[r : r + 8], 0.0), slot[r : r + 8], axis=1
@@ -595,20 +697,20 @@
         return carry
 
     lax.fori_loop(0, 8, expand, 0)
-    small_part[...] = jnp.zeros((16, LATS), F32)
+    small_part[TAPS + 1 :, :] = jnp.zeros((16 - TAPS - 1, LATS), F32)
 
     def correlate(c, carry):
         lanes = pl.ds(pl.multiple_of(c * 128, 128), 128)
         own = dense[:, lanes]
-        wide = lat_ref[:, lanes]
         for k in range(TAPS):
             small_part[k : k + 1, lanes] = jnp.sum(
-                own * wide[k + HALF : k + HALF + TOK], axis=0, keepdims=True
+                own * lat_ref[c, k + HALF : k + HALF + TOK, :], axis=0, keepdims=True
             )
         small_part[TAPS : TAPS + 1, lanes] = jnp.sum(own, axis=0, keepdims=True)
         return carry
 
     lax.fori_loop(0, 8, correlate, 0)
+    small_out[...] = small_part[...].astype(BF16)
     for delta in range(1, GROUP):
         small_copy(delta).start()
     own_copies = [
@@ -617,16 +719,16 @@
     ]
     for copy in own_copies:
         copy.start()
-    small_in[me] = small_part[...]
+    small_in[me] = small_out[...]
     for copy in own_copies:
         copy.wait()
     for delta in range(1, GROUP):
         code_copy(delta).wait_recv()
         total_copy(delta).wait_recv()
         small_copy(delta).wait_recv()
-    small = small_in[0]
+    small = small_in[0].astype(F32)
     for j in range(1, GROUP):
-        small = small + small_in[j]
+        small = small + small_in[j].astype(F32)
     small_ref[...] = small
     for delta in range(1, GROUP):
         code_copy(delta).wait_send()
@@ -635,61 +737,60 @@
         small_copy(delta).wait_send()
 
 
-def all_codes(latents, res8, dictionary, ids8, own_inv, lat):
+def all_codes(latents, res8, dwin, ids8, own_inv, lat):
     shape = jax.ShapeDtypeStruct((GROUP, 128, 128), BF16)
     dma = pltpu.SemaphoreType.DMA
     return pl.pallas_call(
         codes_kernel,
         out_shape=(shape, shape, jax.ShapeDtypeStruct((16, LATS), F32)),
-        in_specs=[VMEM, VMEM, ANY, VMEM, VMEM, VMEM],
+        in_specs=[VMEM] * 6,
         out_specs=(VMEM, VMEM, VMEM),
         scratch_shapes=[
-            pltpu.VMEM((LATS, WIN), BF16),
             pltpu.VMEM((TOK, LATS), F32),
+            pltpu.VMEM((128, 128), jnp.int32),
             pltpu.VMEM((128, 128), BF16),
             pltpu.VMEM((GROUP, 128, 128), BF16),
             pltpu.VMEM((GROUP, 128, 128), BF16),
             pltpu.VMEM((128, 128), BF16),
             pltpu.VMEM((16, LATS), F32),
-            pltpu.VMEM((GROUP, 16, LATS), F32),
+            pltpu.VMEM((16, LATS), BF16),
+            pltpu.VMEM((GROUP, 16, LATS), BF16),
         ]
         + [dma((7,))] * 8
         + [dma((3,))],
         compiler_params=pltpu.CompilerParams(
-            collective_id=2, has_side_effects=True, vmem_limit_bytes=32 * 1024 * 1024
+            collective_id=2, has_side_effects=True, vmem_limit_bytes=16 * 1024 * 1024
         ),
         name="all_codes",
-    )(latents, res8, dictionary, ids8, own_inv, lat)
+    )(latents, res8, dwin, ids8, own_inv, lat)
 
 
 SEQ_ROWS = 4 * TOK + 16
-UNROLL = 4
+CHUNK = 256
 
 
 def dictionary_kernel(
-    where_ref, inv_ref, codes_ref, grad_ref, res_ref, act_ref, taps_ref,
-    out_ref, dense, pre, grad_in, res_t, act_t, product,
+    where_ref, inv_hbm, codes_hbm, grad_hbm, res_hbm, act_t_hbm, taps_ref,
+    out_ref, inv_ref, codes_ref, grad_ref, res_ref, act_t_ref, dense, pre, grad_in, res_t, product, sems,
 ):
-    width = inv_ref.shape[1]
-    tiles = width // 128
+    sources = [inv_hbm, codes_hbm, grad_hbm, res_hbm, act_t_hbm]
+    targets = [inv_ref, codes_ref, grad_ref, res_ref, act_t_ref]
+    copies = [pltpu.make_async_copy(a, b, sems.at[n]) for n, (a, b) in enumerate(zip(sources, targets))]
+    for n in (1, 2, 0, 3, 4):
+        copies[n].start()
+    tiles = CHUNK // 128
     for c in range(tiles):
         for b in range(2):
             pre[c, b, 0:8, :] = jnp.zeros((8, 128), F32)
             pre[c, b, 8 + 4 * TOK :, :] = jnp.zeros((8, 128), F32)
-
-    @pl.when(pl.program_id(0) == 0)
-    def _():
-        for j in range(GROUP):
-            res_t[:, j * TOK : (j + 1) * TOK] = res_ref[j].T
-            act_t[:, j * TOK : (j + 1) * TOK] = act_ref[j].T
-
     keep = lax.broadcasted_iota(jnp.int32, (16, 128), 1) < SLOTS
-
-    def expand(block):
-        j = block // 8
-        row = pl.multiple_of(lax.rem(block, 8) * 16, 16)
-        codes = codes_ref[j, pl.ds(row, 16), :].astype(F32)
-        grad = grad_ref[j, pl.ds(row, 16), :].astype(F32)
+    for n in (1, 2, 0):
+        copies[n].wait()
+
+    def expand(g, j, u):
+        row = u * 16
+        codes = codes_ref[j, row : row + 16, :].astype(F32)
+        grad = grad_ref[j, row : row + 16, :].astype(F32)
         for side in range(2):
             if side:
                 codes = pltpu.roll(codes, SLOTS, 1)
@@ -697,10 +798,11 @@
             codes_side = jnp.where(keep, codes, 0.0)
             grad_side = jnp.where(keep, grad, 0.0)
             start = pl.multiple_of(j * TOK + side * 128 + row, 16)
+            packed = inv_ref[pl.ds(start, 16), pl.ds(pl.multiple_of((g // 2) * 128, 128), 128)]
             into = pl.multiple_of(8 + (j // 2) * TOK + side * 128 + row, 8)
             for c in range(tiles):
                 at = slice(c * 128, (c + 1) * 128)
-                slot = inv_ref[pl.ds(start, 16), at].astype(F32).astype(jnp.int32)
+                slot = slot_lane(packed, 7 * (lax.rem(g, 2) * 2 + c))
                 wide = [
                     jnp.take_along_axis(codes_side[r : r + 8], slot[r : r + 8], axis=1)
                     for r in (0, 8)
@@ -711,75 +813,85 @@
                         grad_side[r : r + 8], slot[r : r + 8], axis=1
                     )
 
-    def expand_some(step, carry):
-        for u in range(UNROLL):
-            expand(step * UNROLL + u)
-        return carry
-
-    lax.fori_loop(0, 64 // UNROLL, expand_some, 0)
-
-    def spread(block, carry):
-        b, row = block // 16, lax.rem(block, 16) * 64
-        j = (row // TOK) * 2 + b
-        into = pl.multiple_of(j * TOK + lax.rem(row, TOK), 64)
-        for c in range(tiles):
-            at = slice(c * 128, (c + 1) * 128)
-            total = jnp.zeros((64, 128), F32)
-            for k in range(TAPS):
-                total = total + taps_ref[k : k + 1, at] * pre[c, b, pl.ds(row + (8 + HALF - k), 64), :]
-            grad_in[pl.ds(into, 64), at] = total.astype(BF16)
-        return carry
-
-    lax.fori_loop(0, 32, spread, 0)
-    product[...] = jnp.dot(
-        res_t[...], dense[...], preferred_element_type=F32
-    ) + jnp.dot(act_t[...], grad_in[...], preferred_element_type=F32)
-    out_ref[...] = product[pl.ds(pl.multiple_of(where_ref[0], 64), OWN), :]
-
-
-def dictionary_gradient(where, inv, codes8, grad8, res8, cols, taps):
-    width = 256
+    def chunk(g, carry):
+        lanes = pl.multiple_of(g * CHUNK, CHUNK)
+
+        def expand_block(j, carry):
+            for u in range(8):
+                expand(g, j, u)
+            return carry
+
+        lax.fori_loop(0, GROUP, expand_block, 0)
+
+        @pl.when(g == 0)
+        def _():
+            copies[3].wait()
+            copies[4].wait()
+            for j in range(GROUP):
+                res_t[:, j * TOK : (j + 1) * TOK] = res_ref[j].T
+
+
+        def spread(j, carry):
+            into = pl.multiple_of(j * TOK, TOK)
+            for c in range(tiles):
+                taps = taps_ref[:, pl.ds(lanes + c * 128, 128)]
+                for part in range(4):
+                    row = (j // 2) * TOK + part * 64
+                    total = jnp.zeros((64, 128), F32)
+                    for k in range(TAPS):
+                        total = (
+                            total
+                            + taps[k : k + 1]
+                            * pre[c, lax.rem(j, 2), pl.ds(row + (8 + HALF - k), 64), :]
+                        )
+                    grad_in[pl.ds(into + part * 64, 64), c * 128 : (c + 1) * 128] = total.astype(
+                        BF16
+                    )
+            return carry
+
+        lax.fori_loop(0, GROUP, spread, 0)
+        product[...] = jnp.dot(
+            res_t[...], dense[...], preferred_element_type=F32
+        ) + jnp.dot(act_t_ref[...], grad_in[...], preferred_element_type=F32)
+        out_ref[:, pl.ds(lanes, CHUNK)] = product[pl.ds(pl.multiple_of(where_ref[0], 64), OWN), :]
+        return carry
+
+    lax.fori_loop(0, LATS // CHUNK, chunk, 0)
+
+
+def dictionary_gradient(where, inv, codes8, grad8, res8, act_t, taps):
     return pl.pallas_call(
         dictionary_kernel,
-        grid=(LATS // width,),
         out_shape=jax.ShapeDtypeStruct((OWN, LATS), F32),
-        in_specs=[
-            pl.BlockSpec(memory_space=pltpu.SMEM),
-            pl.BlockSpec((GROUP * TOK, width), lambda i: (0, i)),
-            pl.BlockSpec((GROUP, 128, 128), lambda i: (0, 0, 0)),
-            pl.BlockSpec((GROUP, 128, 128), lambda i: (0, 0, 0)),
-            pl.BlockSpec((GROUP, TOK, WIN), lambda i: (0, 0, 0)),
-            pl.BlockSpec((GROUP, TOK, WIN), lambda i: (0, 0, 0)),
-            pl.BlockSpec((TAPS, width), lambda i: (0, i)),
+        in_specs=[pl.BlockSpec(memory_space=pltpu.SMEM)] + [ANY] * 5 + [VMEM],
+        out_specs=VMEM,
+        scratch_shapes=[
+            pltpu.VMEM((GROUP * TOK, 256), jnp.int32),
+            pltpu.VMEM((GROUP, 128, 128), BF16),
+            pltpu.VMEM((GROUP, 128, 128), BF16),
+            pltpu.VMEM((GROUP, TOK, WIN), BF16),
+            pltpu.VMEM((WIN, GROUP * TOK), BF16),
+            pltpu.VMEM((GROUP * TOK, CHUNK), BF16),
+            pltpu.VMEM((CHUNK // 128, 2, SEQ_ROWS, 128), F32),
+            pltpu.VMEM((GROUP * TOK, CHUNK), BF16),
+            pltpu.VMEM((WIN, GROUP * TOK), BF16),
+            pltpu.VMEM((WIN, CHUNK), F32),
+            pltpu.SemaphoreType.DMA((5,)),
         ],
-        out_specs=pl.BlockSpec((OWN, width), lambda i: (0, i)),
-        scratch_shapes=[
-            pltpu.VMEM((GROUP * TOK, width), BF16),
-            pltpu.VMEM((width // 128, 2, SEQ_ROWS, 128), F32),
-            pltpu.VMEM((GROUP * TOK, width), BF16),
-            pltpu.VMEM((WIN, GROUP * TOK), BF16),
-            pltpu.VMEM((WIN, GROUP * TOK), BF16),
-            pltpu.VMEM((WIN, width), F32),
-        ],
+        compiler_params=pltpu.CompilerParams(vmem_limit_bytes=61 * 1024 * 1024),
         name="dictionary_gradient",
-    )(where, inv, codes8, grad8, res8, cols, taps)
+    )(where, inv, codes8, grad8, res8, act_t, taps)
 
 
 def body(activations, dictionary, topk_ids, kernel_taps, enc_bias):
     act = activations[0]
-    ids = topk_ids[0]
-    ids = jnp.concatenate([ids[:128], ids[128:]], axis=1)
-    lat, own_inv, ids8 = opening(act, dictionary, ids)
-    preact = jnp.zeros((TOK, LATS), F32)
-    for k in range(TAPS):
-        preact = preact + kernel_taps[k][None, :] * lat[k + HALF : k + HALF + TOK]
-    preact = preact + enc_bias[None, :]
-    latents = jnp.where(own_inv < NONE, preact, 0.0).astype(BF16)
-    part = jnp.einsum("tl,ld->td", latents, dictionary, preferred_element_type=F32).astype(BF16)
-    res8, cols, inv = summed(part, act, ids8, own_inv)
-    grad8, codes8, small = all_codes(latents, res8, dictionary, ids8, own_inv, lat)
+    latents, part, dwin, lat, own_inv, ids8 = opening(
+        act, dictionary, topk_ids[0].T, kernel_taps, enc_bias[None]
+    )
+    res8, act_t, inv = summed(part, act, ids8, own_inv)
+    grad8, codes8, small = all_codes(latents, res8, dwin, ids8, own_inv, lat)
     where = (lax.axis_index("batch") * 64).astype(jnp.int32)[None]
-    gradient = dictionary_gradient(where, inv, codes8, grad8, res8, cols, kernel_taps)
+    gradient = dictionary_gradient(where, inv, codes8, grad8, res8, act_t, kernel_taps)
     return gradient.T, small[:TAPS], small[TAPS]
 
 

time: 142 us -> 129 us (0.908)
  Pallas kernels: 127 us -> 120 us
  matrix products: 2.06 us -> 0 us
  local copies, waits for them, and re-layouts: 9.44 us -> 7.81 us
  other arithmetic: 1.43 us -> 0 us
    pallas_call x1, Pallas kernels: 61.5 us -> 52.1 us  [summed(): pl.pallas_call(sum_kernel, out_shape=(jax.ShapeDtypeStruct((GROUP, TOK, W...]
    pallas_call x2, Pallas kernels: 42.7 us -> 46 us  [the longest x1 28.1 us: dictionary_gradient(): pl.pallas_call(dictionary_kernel, out_shape=jax.ShapeDtypeStruct((OWN, LA...]
    dot_general x1 -> x0, matrix products: 2.06 us -> none  [body(): jnp.einsum('tl,ld->td', latents, dictionary, preferred_element_type=F32)]
    slice x2 -> x0, local copies, waits for them, and re-layouts: 1.98 us -> none  [the longest x1 1.2 us: body(): preact = preact + kernel_taps[k][None, :] * lat[k + HALF:k + HALF + TOK]]
    unnamed x25 -> x21, local copies, waits for them, and re-layouts: 6.86 us -> 7.21 us
where the time goes in v3:
time: 129 us
  Pallas kernels  120 us (93%)
  local copies, waits for them, and re-layouts  7.81 us (6%)
    pallas_call x1, Pallas kernels, summed(): pl.pallas_call(sum_kernel, out_shape=(jax.ShapeDtypeStruct((GROUP, TOK, W...  52.1 us
    pallas_call x1, Pallas kernels, dictionary_gradient(): pl.pallas_call(dictionary_kernel, out_shape=jax.ShapeDtypeStruct((OWN, LA...  28.1 us
    pallas_call x1, Pallas kernels, all_codes(): pl.pallas_call(codes_kernel, out_shape=(shape, shape, jax.ShapeDtypeStruc...  22 us
    pallas_call x1, Pallas kernels, opening(): pl.pallas_call(opening_kernel, out_shape=(jax.ShapeDtypeStruct((TOK, LATS...  17.8 us
    unnamed x21, local copies, waits for them, and re-layouts  7.21 us

profile of v3, /device:TPU:32, one launch (start us, length us, event | category | flops | bytes accessed | tf_op | source)
XLA Modules:
  0.0 128.6 jit_solution(8899267359627096925)
XLA Ops:
  0.6 0.0 copy-start.5
  0.6 0.8 copy-done.5
  1.5 0.0 copy-start.8
  1.5 0.8 copy-done.8
  2.3 0.0 copy-start.9
  2.3 0.7 copy-done.9
  3.0 0.0 copy-start.1
  3.0 17.8 %opening.1 = (bf16[256,1024]{1,0:T(8,128)(2,1)S(1)}, bf16[256,3584]{1,0:T(8,128)(2,1)}, bf16[1024,512]{1,0:T(8,128)(2,1)S(1)}, f32[8,272,128]{2,1,0:T(8,128)S(1)...) custom-call(bf16[256,3584]{1,0:T(8,128)(2,1)} %bitcast.9, bf16[1024,3584]{1,0:T(8,128)(2,1)} %dict_ref.1, ...), custom_call_target="tpu_custom_call" | custom-call | tf_op jit(solution)/shard_map/opening/pallas_call | solution.py:223
  20.9 0.0 copy-done.1
  20.9 0.0 copy-start.4
  20.9 1.5 %copy-done.4 = bf16[256,3584]{1,0:T(8,128)(2,1)S(1)} copy-done((bf16[256,3584]{1,0:T(8,128)(2,1)S(1)}, bf16[256,3584]{1,0:T(8,128)(2,1)}, u32[]{:S(2)}) %copy-start.4) | copy-done | bytes 1835032
  22.4 52.1 %summed.1 = (bf16[8,256,512]{2,1,0:T(8,128)(2,1)S(1)}, bf16[512,2048]{1,0:T(8,128)(2,1)S(1)}, s32[2048,256]{1,0:T(8,128)S(1)}) custom-call(bf16[256,3584]{1,0:T(8,128)(2,1)S(1)} %copy-done.4, bf16[256,3584]{1,0:T(8,128)(2,1)S(1)} %bitcast.10, s32[8,64,256]{2,1,0:T(8,128)S(1)} %get-tuple-element.16.ids8_ref, s32[256,256]{1,0:T(8,128)S(1)} %get-tuple-element.17.own_inv_ref.inv_ref), custom_call_target="tpu_custom_call" | custom-call | tf_op jit(solution)/shard_map/summed/pallas_call | solution.py:534
  74.5 0.0 copy-start.3
  74.5 1.3 %copy-done.3 = s32[2048,256]{1,0:T(8,128)} copy-done((s32[2048,256]{1,0:T(8,128)}, s32[2048,256]{1,0:T(8,128)S(1)}, u32[]{:S(2)}) %copy-start.3) | copy-done | bytes 2097176
  75.8 0.0 copy-start
  75.8 0.0 copy-start.2
  75.8 22.0 %all_codes.1 = (bf16[8,128,128]{2,1,0:T(8,128)(2,1)S(1)}, bf16[8,128,128]{2,1,0:T(8,128)(2,1)S(1)}, f32[16,1024]{1,0:T(8,128)S(1)}) custom-call(bf16[256,1024]{1,0:T(8,128)(2,1)S(1)} %get-tuple-element.19.latents_ref, bf16[8,256,512]{2,1,0:T(8,128)(2,1)S(1)} %get-tuple-element.20.res8_ref.res_hbm, bf16[1024,512]{1,0:T(8,128)(2,1)S(1)} %get-tuple-element.21.dwin, ...), custom_call_target="tpu_custom_call" | custom-call | tf_op jit(solution)/shard_map/all_codes/pallas_call | solution.py:743
  97.8 0.0 copy-done
  97.8 0.0 copy-done.2
  97.8 0.0 copy-start.6
  97.8 0.7 copy-done.6
  98.5 0.0 copy-start.7
  98.5 0.7 copy-done.7
  99.2 28.1 %dictionary_gradient.1 = f32[448,1024]{1,0:T(8,128)} custom-call(s32[1]{0:T(128)} %bitcast.where_ref, s32[2048,256]{1,0:T(8,128)} %copy-done.3, bf16[8,128,128]{2,1,0:T(8,128)(2,1)} %copy-done.7, bf16[8,128,128]{2,1,0:T(8,128)(2,1)} %copy-done.6, bf16[8,256,512]{2,1,0:T(8,128)(2,1)} %copy-done, bf16[512,2048]{1,0:T(8,128)(2,1)} %copy-done.2, f32[9,1024]{1,0:T(8,128)} %taps_ref.1), custom_call_target="tpu_custom_call" | custom-call | tf_op jit(solution)/shard_map/dictionary_gradient/pallas_call | solution.py:863
  127.3 0.6 slice.7
  127.9 0.6 copy.9
Async XLA Ops:
  0.6 0.8 copy-start.5
  1.5 0.8 copy-start.8
  2.3 0.7 copy-start.9
  3.0 17.9 %copy-start.1 = (bf16[1,256,3584]{2,1,0:T(8,128)(2,1)S(1)}, bf16[1,256,3584]{2,1,0:T(8,128)(2,1)}, u32[]{:S(2)}) copy-start(bf16[1,256,3584]{2,1,0:T(8,128)(2,1)} %param.5) | copy-start | bytes 5505028
  20.9 1.5 %copy-start.4 = (bf16[256,3584]{1,0:T(8,128)(2,1)S(1)}, bf16[256,3584]{1,0:T(8,128)(2,1)}, u32[]{:S(2)}) copy-start(bf16[256,3584]{1,0:T(8,128)(2,1)} %get-tuple-element.15.part_ref) | copy-start | bytes 5505028
  74.5 1.3 %copy-start.3 = (s32[2048,256]{1,0:T(8,128)}, s32[2048,256]{1,0:T(8,128)S(1)}, u32[]{:S(2)}) copy-start(s32[2048,256]{1,0:T(8,128)S(1)} %get-tuple-element.18.inv_hbm) | copy-start | bytes 6291460
  75.8 22.0 %copy-start = (bf16[8,256,512]{2,1,0:T(8,128)(2,1)}, bf16[8,256,512]{2,1,0:T(8,128)(2,1)S(1)}, u32[]{:S(2)}) copy-start(bf16[8,256,512]{2,1,0:T(8,128)(2,1)S(1)} %get-tuple-element.20.res8_ref.res_hbm) | copy-start | bytes 6291460
  75.8 22.0 %copy-start.2 = (bf16[512,2048]{1,0:T(8,128)(2,1)}, bf16[512,2048]{1,0:T(8,128)(2,1)S(1)}, u32[]{:S(2)}) copy-start(bf16[512,2048]{1,0:T(8,128)(2,1)S(1)} %get-tuple-element.25.act_t_hbm) | copy-start | bytes 6291460
  97.8 0.7 copy-start.6
  98.5 0.7 copy-start.7

commit v4 on v3

--- a/solution.py
+++ b/solution.py
@@ -25,6 +25,9 @@
 VMEM = pl.BlockSpec(memory_space=pltpu.VMEM)
 ANY = pl.BlockSpec(memory_space=pl.ANY)
 OPENING_MIB = 50
+SUM_MIB = 52
+CODES_MIB = 50
+LAST_MIB = 50
 
 
 def seat():
@@ -254,8 +257,8 @@
 
 
 def sum_kernel(
-    part_ref, act_ref, ids8_ref, own_inv_ref, res8_ref, act_t_ref, inv_ref,
-    cols_ref, rows_ref, found_ref, half, down_out, down_in, up_out, up_in, own_sum, other_sum, res, slices,
+    part_hbm, act_hbm, ids8_ref, own_inv_ref, res8_ref, act_t_hbm, inv_hbm,
+    part_ref, act_t_ref, inv_ref, act_ref, cols_ref, rows_ref, found_ref, half, down_out, down_in, up_out, up_in, own_sum, other_sum, res, slices,
     half_sem, dsend, drecv, usend, urecv, xsend, xrecv, asend, arecv,
     gdsend, gdrecv, gusend, gurecv, csend, crecv, act_send, act_recv, swap_send, swap_recv, own_sem,
 ):
@@ -289,10 +292,13 @@
         own_inv_ref, inv_ref.at[pl.ds(pl.multiple_of(me * TOK, TOK), TOK)], own_sem.at[0]
     )
     own_inv.start()
+    act_in = pltpu.make_async_copy(act_hbm, act_ref, own_sem.at[3])
+    part_in = pltpu.make_async_copy(part_hbm, part_ref, own_sem.at[4])
+    part_in.start()
+    act_in.start()
     own_cols = pltpu.make_async_copy(
         act_ref.at[:, pl.ds(window(me), WIN)], cols_ref.at[me], own_sem.at[1]
     )
-    own_cols.start()
     enter([other_core, below, above, other_x] + group_partners())
 
     def half_copy():
@@ -316,7 +322,10 @@
             rows_here, rows_here, swap_send.at[delta - 1], swap_recv.at[delta - 1], other_core
         )
 
+    part_in.wait()
     half_copy().start()
+    act_in.wait()
+    own_cols.start()
     for delta in range(1, GROUP):
         act_copy(delta).start()
     work_many(0, 3)
@@ -496,6 +505,11 @@
         return carry
 
     lax.fori_loop(0, 12, next_regions, 0)
+    own_inv.wait()
+    act_t_out = pltpu.make_async_copy(act_t_ref, act_t_hbm, own_sem.at[5])
+    inv_out = pltpu.make_async_copy(inv_ref, inv_hbm, own_sem.at[6])
+    act_t_out.start()
+    inv_out.start()
     for h in range(4):
         arrived(gdrecv.at[3, h], lax.rem(z + 4, 8), h)
     core_copy(lax.rem(z + 4, 8), 4).start()
@@ -503,7 +517,8 @@
         chunk = lax.rem(z + n, 8) if n < 5 else lax.rem(z + 12 - n, 8)
         part = chunk_rows(give, chunk)
         pltpu.make_async_copy(part, part, crecv.at[n]).wait()
-    own_inv.wait()
+    act_t_out.wait()
+    inv_out.wait()
     for delta in range(1, GROUP):
         act_copy(delta).wait_send()
         swap_copy(delta).wait_send()
@@ -538,9 +553,13 @@
             jax.ShapeDtypeStruct((WIN, GROUP * TOK), BF16),
             jax.ShapeDtypeStruct((GROUP * TOK, 256), jnp.int32),
         ),
-        in_specs=[VMEM] * 4,
-        out_specs=[VMEM] * 3,
+        in_specs=[ANY, ANY, VMEM, VMEM],
+        out_specs=[VMEM, ANY, ANY],
         scratch_shapes=[
+            pltpu.VMEM((TOK, D), BF16),
+            pltpu.VMEM((WIN, GROUP * TOK), BF16),
+            pltpu.VMEM((GROUP * TOK, 256), jnp.int32),
+            pltpu.VMEM((TOK, D), BF16),
             pltpu.VMEM((GROUP, TOK, WIN), BF16),
             *SLOT_SCRATCH,
             pltpu.VMEM((128, D), BF16),
@@ -571,10 +590,10 @@
             dma((7,)),
             dma((7,)),
             dma((7,)),
-            dma((3,)),
+            dma((7,)),
         ],
         compiler_params=pltpu.CompilerParams(
-            collective_id=1, has_side_effects=True, vmem_limit_bytes=24 * 1024 * 1024
+            collective_id=1, has_side_effects=True, vmem_limit_bytes=SUM_MIB * 1024 * 1024
         ),
         name="summed",
     )(part, act, ids8, own_inv)
@@ -615,13 +634,15 @@
 
 
 def codes_kernel(
-    latents_ref, res8_ref, dwin, ids8_ref, inv_ref, lat_ref,
+    latents_ref, res8_hbm, dwin, ids8_ref, inv_ref, lat_ref,
     total_ref, codes8_ref, small_ref,
-    dense, ids_rows, codes, part, arrived, own_total, small_part, small_out, small_in,
+    res8_ref, dense, ids_rows, codes, part, arrived, own_total, small_part, small_out, small_in,
     psend, precv, csend, crecv, tsend, trecv, ssend, srecv, own_sem,
 ):
     me = seat()
     first = first_latent()
+    res_in = pltpu.make_async_copy(res8_hbm, res8_ref, own_sem.at[0])
+    res_in.start()
     dense[...] = latents_ref[...].astype(F32)
 
     def rows_of(j):
@@ -653,6 +674,7 @@
 
     for delta in range(1, GROUP):
         code_copy(delta).start()
+    res_in.wait()
 
     def block(n, carry):
         j = lax.rem(me + n, GROUP)
@@ -743,9 +765,10 @@
     return pl.pallas_call(
         codes_kernel,
         out_shape=(shape, shape, jax.ShapeDtypeStruct((16, LATS), F32)),
-        in_specs=[VMEM] * 6,
+        in_specs=[VMEM, ANY] + [VMEM] * 4,
         out_specs=(VMEM, VMEM, VMEM),
         scratch_shapes=[
+            pltpu.VMEM((GROUP, TOK, WIN), BF16),
             pltpu.VMEM((TOK, LATS), F32),
             pltpu.VMEM((128, 128), jnp.int32),
             pltpu.VMEM((128, 128), BF16),
@@ -759,7 +782,7 @@
         + [dma((7,))] * 8
         + [dma((3,))],
         compiler_params=pltpu.CompilerParams(
-            collective_id=2, has_side_effects=True, vmem_limit_bytes=16 * 1024 * 1024
+            collective_id=2, has_side_effects=True, vmem_limit_bytes=CODES_MIB * 1024 * 1024
         ),
         name="all_codes",
     )(latents, res8, dwin, ids8, own_inv, lat)
@@ -770,22 +793,23 @@
 
 
 def dictionary_kernel(
-    where_ref, inv_hbm, codes_hbm, grad_hbm, res_hbm, act_t_hbm, taps_ref,
-    out_ref, inv_ref, codes_ref, grad_ref, res_ref, act_t_ref, dense, pre, grad_in, res_t, product, sems,
+    where_ref, inv_hbm, res_hbm, act_t_hbm, codes_ref, grad_ref, taps_ref, small_ref,
+    out_ref, taps_out_ref, bias_out_ref, inv_ref, res_ref, act_t_ref, dense, pre, grad_in, res_t, product, sems,
 ):
-    sources = [inv_hbm, codes_hbm, grad_hbm, res_hbm, act_t_hbm]
-    targets = [inv_ref, codes_ref, grad_ref, res_ref, act_t_ref]
+    sources = [inv_hbm, res_hbm, act_t_hbm]
+    targets = [inv_ref, res_ref, act_t_ref]
     copies = [pltpu.make_async_copy(a, b, sems.at[n]) for n, (a, b) in enumerate(zip(sources, targets))]
-    for n in (1, 2, 0, 3, 4):
-        copies[n].start()
+    for copy in copies:
+        copy.start()
+    taps_out_ref[...] = small_ref[:TAPS, :]
+    bias_out_ref[...] = small_ref[TAPS : TAPS + 1, :]
     tiles = CHUNK // 128
     for c in range(tiles):
         for b in range(2):
             pre[c, b, 0:8, :] = jnp.zeros((8, 128), F32)
             pre[c, b, 8 + 4 * TOK :, :] = jnp.zeros((8, 128), F32)
     keep = lax.broadcasted_iota(jnp.int32, (16, 128), 1) < SLOTS
-    for n in (1, 2, 0):
-        copies[n].wait()
+    copies[0].wait()
 
     def expand(g, j, u):
         row = u * 16
@@ -825,8 +849,8 @@
 
         @pl.when(g == 0)
         def _():
-            copies[3].wait()
-            copies[4].wait()
+            copies[1].wait()
+            copies[2].wait()
             for j in range(GROUP):
                 res_t[:, j * TOK : (j + 1) * TOK] = res_ref[j].T
 
@@ -859,16 +883,18 @@
     lax.fori_loop(0, LATS // CHUNK, chunk, 0)
 
 
-def dictionary_gradient(where, inv, codes8, grad8, res8, act_t, taps):
+def dictionary_gradient(where, inv, res8, act_t, codes8, grad8, taps, small):
     return pl.pallas_call(
         dictionary_kernel,
-        out_shape=jax.ShapeDtypeStruct((OWN, LATS), F32),
-        in_specs=[pl.BlockSpec(memory_space=pltpu.SMEM)] + [ANY] * 5 + [VMEM],
-        out_specs=VMEM,
+        out_shape=(
+            jax.ShapeDtypeStruct((OWN, LATS), F32),
+            jax.ShapeDtypeStruct((TAPS, LATS), F32),
+            jax.ShapeDtypeStruct((1, LATS), F32),
+        ),
+        in_specs=[pl.BlockSpec(memory_space=pltpu.SMEM)] + [ANY] * 3 + [VMEM] * 4,
+        out_specs=(VMEM, VMEM, VMEM),
         scratch_shapes=[
             pltpu.VMEM((GROUP * TOK, 256), jnp.int32),
-            pltpu.VMEM((GROUP, 128, 128), BF16),
-            pltpu.VMEM((GROUP, 128, 128), BF16),
             pltpu.VMEM((GROUP, TOK, WIN), BF16),
             pltpu.VMEM((WIN, GROUP * TOK), BF16),
             pltpu.VMEM((GROUP * TOK, CHUNK), BF16),
@@ -876,11 +902,11 @@
             pltpu.VMEM((GROUP * TOK, CHUNK), BF16),
             pltpu.VMEM((WIN, GROUP * TOK), BF16),
             pltpu.VMEM((WIN, CHUNK), F32),
-            pltpu.SemaphoreType.DMA((5,)),
+            pltpu.SemaphoreType.DMA((3,)),
         ],
-        compiler_params=pltpu.CompilerParams(vmem_limit_bytes=61 * 1024 * 1024),
+        compiler_params=pltpu.CompilerParams(vmem_limit_bytes=LAST_MIB * 1024 * 1024),
         name="dictionary_gradient",
-    )(where, inv, codes8, grad8, res8, act_t, taps)
+    )(where, inv, res8, act_t, codes8, grad8, taps, small)
 
 
 def body(activations, dictionary, topk_ids, kernel_taps, enc_bias):
@@ -891,8 +917,10 @@
     res8, act_t, inv = summed(part, act, ids8, own_inv)
     grad8, codes8, small = all_codes(latents, res8, dwin, ids8, own_inv, lat)
     where = (lax.axis_index("batch") * 64).astype(jnp.int32)[None]
-    gradient = dictionary_gradient(where, inv, codes8, grad8, res8, act_t, kernel_taps)
-    return gradient.T, small[:TAPS], small[TAPS]
+    gradient, grad_taps, grad_bias = dictionary_gradient(
+        where, inv, res8, act_t, codes8, grad8, kernel_taps, small
+    )
+    return gradient.T, grad_taps, grad_bias[0]
 
 
 def solution(mesh):

time: 129 us -> 122 us (0.946)
  local copies, waits for them, and re-layouts: 7.81 us -> 2.37 us
    unnamed x21 -> x10, local copies, waits for them, and re-layouts: 7.21 us -> 2.37 us
    pallas_call x1, Pallas kernels: 28.1 us -> 25.6 us  [dictionary_gradient(): pl.pallas_call(dictionary_kernel, out_shape=(jax.ShapeDtypeStruct((OWN, L...]
    pallas_call x1, Pallas kernels: 52.1 us -> 53.8 us  [summed(): pl.pallas_call(sum_kernel, out_shape=(jax.ShapeDtypeStruct((GROUP, TOK, W...]
where the time goes in v4:
time: 122 us
  Pallas kernels  119 us (98%)
  local copies, waits for them, and re-layouts  2.37 us (2%)
    pallas_call x1, Pallas kernels, summed(): pl.pallas_call(sum_kernel, out_shape=(jax.ShapeDtypeStruct((GROUP, TOK, W...  53.8 us
    pallas_call x1, Pallas kernels, dictionary_gradient(): pl.pallas_call(dictionary_kernel, out_shape=(jax.ShapeDtypeStruct((OWN, L...  25.6 us
    pallas_call x1, Pallas kernels, all_codes(): pl.pallas_call(codes_kernel, out_shape=(shape, shape, jax.ShapeDtypeStruc...  22 us
    pallas_call x1, Pallas kernels, opening(): pl.pallas_call(opening_kernel, out_shape=(jax.ShapeDtypeStruct((TOK, LATS...  17.7 us

profile of v4, /device:TPU:32, one launch (start us, length us, event | category | flops | bytes accessed | tf_op | source)
XLA Modules:
  0.0 122.2 jit_solution(12389189509833585946)
XLA Ops:
  0.6 0.0 copy-start.1
  0.6 0.8 copy-done.1
  1.5 0.0 copy-start.3
  1.5 0.8 copy-done.3
  2.3 0.0 copy-start.4
  2.3 0.7 copy-done.4
  3.0 17.7 %opening.1 = (bf16[256,1024]{1,0:T(8,128)(2,1)S(1)}, bf16[256,3584]{1,0:T(8,128)(2,1)}, bf16[1024,512]{1,0:T(8,128)(2,1)S(1)}, f32[8,272,128]{2,1,0:T(8,128)S(1)...) custom-call(bf16[256,3584]{1,0:T(8,128)(2,1)} %bitcast.10, bf16[1024,3584]{1,0:T(8,128)(2,1)} %dict_ref.1, ...), custom_call_target="tpu_custom_call" | custom-call | tf_op jit(solution)/shard_map/opening/pallas_call | solution.py:226
  20.7 53.8 %summed.1 = (bf16[8,256,512]{2,1,0:T(8,128)(2,1)}, bf16[512,2048]{1,0:T(8,128)(2,1)}, s32[2048,256]{1,0:T(8,128)}) custom-call(bf16[256,3584]{1,0:T(8,128)(2,1)} %get-tuple-element.18.part_hbm, bf16[256,3584]{1,0:T(8,128)(2,1)} %bitcast.11, s32[8,64,256]{2,1,0:T(8,128)S(1)} %get-tuple-element.19.ids8_ref, s32[256,256]{1,0:T(8,128)S(1)} %get-tuple-element.20.own_inv_ref.inv_ref), custom_call_target="tpu_custom_call" | custom-call | tf_op jit(solution)/shard_map/summed/pallas_call | solution.py:549
  74.5 0.0 copy-start
  74.5 0.0 copy-start.2
  74.5 22.0 %all_codes.1 = (bf16[8,128,128]{2,1,0:T(8,128)(2,1)S(1)}, bf16[8,128,128]{2,1,0:T(8,128)(2,1)S(1)}, f32[16,1024]{1,0:T(8,128)S(1)}) custom-call(bf16[256,1024]{1,0:T(8,128)(2,1)S(1)} %get-tuple-element.24.latents_ref, bf16[8,256,512]{2,1,0:T(8,128)(2,1)} %get-tuple-element.22.res8_hbm.res_hbm, bf16[1024,512]{1,0:T(8,128)(2,1)S(1)} %get-tuple-element.25.dwin, ...), custom_call_target="tpu_custom_call" | custom-call | tf_op jit(solution)/shard_map/all_codes/pallas_call | solution.py:765
  96.6 0.0 copy-done
  96.6 0.0 copy-done.2
  96.6 25.6 %dictionary_gradient.1 = (f32[448,1024]{1,0:T(8,128)}, f32[9,1024]{1,0:T(8,128)}, f32[1,1024]{1,0:T(1,128)}) custom-call(s32[1]{0:T(128)} %bitcast.where_ref, s32[2048,256]{1,0:T(8,128)S(1)} %copy-done, bf16[8,256,512]{2,1,0:T(8,128)(2,1)} %get-tuple-element.22.res8_hbm.res_hbm, bf16[512,2048]{1,0:T(8,128)(2,1)} %get-tuple-element.23.act_t_hbm, ...), custom_call_target="tpu_custom_call" | custom-call | tf_op jit(solution)/shard_map/dictionary_gradient/pallas_call | solution.py:887
Async XLA Ops:
  0.6 0.8 copy-start.1
  1.5 0.8 copy-start.3
  2.3 0.7 copy-start.4
  74.5 22.1 %copy-start = (s32[2048,256]{1,0:T(8,128)S(1)}, s32[2048,256]{1,0:T(8,128)}, u32[]{:S(2)}) copy-start(s32[2048,256]{1,0:T(8,128)} %get-tuple-element.21.inv_hbm) | copy-start | bytes 6291460
  74.5 22.1 %copy-start.2 = (f32[9,1024]{1,0:T(8,128)S(1)}, f32[9,1024]{1,0:T(8,128)}, u32[]{:S(2)}) copy-start(f32[9,1024]{1,0:T(8,128)} %taps_ref.1) | copy-start | bytes 110596

commit v5 on v4

--- a/solution.py
+++ b/solution.py
@@ -299,7 +299,12 @@
     own_cols = pltpu.make_async_copy(
         act_ref.at[:, pl.ds(window(me), WIN)], cols_ref.at[me], own_sem.at[1]
     )
-    enter([other_core, below, above, other_x] + group_partners())
+    partners = [other_core, below, above, other_x] + group_partners()
+    barrier = pltpu.get_barrier_semaphore()
+    for device in partners:
+        pl.semaphore_signal(barrier, inc=1, device_id=device, device_id_type=MESH)
+    work_many(0, 4)
+    pl.semaphore_wait(barrier, len(partners))
 
     def half_copy():
         return remote(
@@ -328,7 +333,7 @@
     own_cols.start()
     for delta in range(1, GROUP):
         act_copy(delta).start()
-    work_many(0, 3)
+    work_many(4, 7)
     half_copy().wait_recv()
     width = D // PIECES
 
@@ -375,7 +380,7 @@
 
     def near_sums(i, carry):
         s, h = i // PIECES + 1, lax.rem(i, PIECES)
-        work(3 + i)
+        work(7 + i)
         down_copy(s - 1, h).wait_recv()
         down_out[s, :, cols_of(h)] = (
             mine(lax.rem(z + 4 + s, 8), h) + down_in[s - 1, :, cols_of(h)].astype(F32)
@@ -404,7 +409,7 @@
         return carry
 
     lax.fori_loop(0, PIECES, last_sums, 0)
-    work_many(15, 20)
+    work_many(19, 24)
     for h in range(PIECES):
         x_copy(h).wait_recv()
     res[...] = (own_sum[...].astype(F32) + other_sum[...].astype(F32)) - act_ref[
@@ -430,7 +435,7 @@
         slice_copy(delta).start()
     own = pltpu.make_async_copy(slices.at[me], res8_ref.at[me, pl.ds(rows, 16)], own_sem.at[2])
     own.start()
-    work_many(20, 24)
+    work_many(24, 28)
     for delta in range(1, GROUP):
         act_copy(delta).wait_recv()
         swap_copy(delta).start()
@@ -471,10 +476,6 @@
 
     def next_regions(i, carry):
         s, h = i // 4 + 1, lax.rem(i, 4)
-
-        @pl.when(i < 4)
-        def _():
-            work(24 + i)
 
         @pl.when(i == 4)
         def _():

time: 122 us -> 122 us (level)
  no operation moved by 1% of the time
where the time goes in v5:
time: 122 us
  Pallas kernels  119 us (98%)
  local copies, waits for them, and re-layouts  2.37 us (2%)
    pallas_call x1, Pallas kernels, summed(): pl.pallas_call(sum_kernel, out_shape=(jax.ShapeDtypeStruct((GROUP, TOK, W...  53.7 us
    pallas_call x1, Pallas kernels, dictionary_gradient(): pl.pallas_call(dictionary_kernel, out_shape=(jax.ShapeDtypeStruct((OWN, L...  25.6 us
    pallas_call x1, Pallas kernels, all_codes(): pl.pallas_call(codes_kernel, out_shape=(shape, shape, jax.ShapeDtypeStruc...  22.1 us
    pallas_call x1, Pallas kernels, opening(): pl.pallas_call(opening_kernel, out_shape=(jax.ShapeDtypeStruct((TOK, LATS...  17.7 us

profile of v5, /device:TPU:32, one launch (start us, length us, event | category | flops | bytes accessed | tf_op | source)
XLA Modules:
  0.0 122.2 jit_solution(10871920577512035260)
XLA Ops:
  0.6 0.0 copy-start.1
  0.6 0.8 copy-done.1
  1.5 0.0 copy-start.3
  1.5 0.8 copy-done.3
  2.3 0.0 copy-start.4
  2.3 0.7 copy-done.4
  3.0 17.7 %opening.1 = (bf16[256,1024]{1,0:T(8,128)(2,1)S(1)}, bf16[256,3584]{1,0:T(8,128)(2,1)}, bf16[1024,512]{1,0:T(8,128)(2,1)S(1)}, f32[8,272,128]{2,1,0:T(8,128)S(1)...) custom-call(bf16[256,3584]{1,0:T(8,128)(2,1)} %bitcast.10, bf16[1024,3584]{1,0:T(8,128)(2,1)} %dict_ref.1, ...), custom_call_target="tpu_custom_call" | custom-call | tf_op jit(solution)/shard_map/opening/pallas_call | solution.py:226
  20.7 53.7 %summed.1 = (bf16[8,256,512]{2,1,0:T(8,128)(2,1)}, bf16[512,2048]{1,0:T(8,128)(2,1)}, s32[2048,256]{1,0:T(8,128)}) custom-call(bf16[256,3584]{1,0:T(8,128)(2,1)} %get-tuple-element.18.part_hbm, bf16[256,3584]{1,0:T(8,128)(2,1)} %bitcast.11, s32[8,64,256]{2,1,0:T(8,128)S(1)} %get-tuple-element.19.ids8_ref, s32[256,256]{1,0:T(8,128)S(1)} %get-tuple-element.20.own_inv_ref.inv_ref), custom_call_target="tpu_custom_call" | custom-call | tf_op jit(solution)/shard_map/summed/pallas_call | solution.py:550
  74.3 0.0 copy-start
  74.3 0.0 copy-start.2
  74.4 22.1 %all_codes.1 = (bf16[8,128,128]{2,1,0:T(8,128)(2,1)S(1)}, bf16[8,128,128]{2,1,0:T(8,128)(2,1)S(1)}, f32[16,1024]{1,0:T(8,128)S(1)}) custom-call(bf16[256,1024]{1,0:T(8,128)(2,1)S(1)} %get-tuple-element.24.latents_ref, bf16[8,256,512]{2,1,0:T(8,128)(2,1)} %get-tuple-element.22.res8_hbm.res_hbm, bf16[1024,512]{1,0:T(8,128)(2,1)S(1)} %get-tuple-element.25.dwin, ...), custom_call_target="tpu_custom_call" | custom-call | tf_op jit(solution)/shard_map/all_codes/pallas_call | solution.py:766
  96.5 0.0 copy-done
  96.5 0.0 copy-done.2
  96.5 25.6 %dictionary_gradient.1 = (f32[448,1024]{1,0:T(8,128)}, f32[9,1024]{1,0:T(8,128)}, f32[1,1024]{1,0:T(1,128)}) custom-call(s32[1]{0:T(128)} %bitcast.where_ref, s32[2048,256]{1,0:T(8,128)S(1)} %copy-done, bf16[8,256,512]{2,1,0:T(8,128)(2,1)} %get-tuple-element.22.res8_hbm.res_hbm, bf16[512,2048]{1,0:T(8,128)(2,1)} %get-tuple-element.23.act_t_hbm, ...), custom_call_target="tpu_custom_call" | custom-call | tf_op jit(solution)/shard_map/dictionary_gradient/pallas_call | solution.py:888
Async XLA Ops:
  0.6 0.8 copy-start.1
  1.5 0.8 copy-start.3
  2.3 0.7 copy-start.4
  74.3 22.2 %copy-start = (s32[2048,256]{1,0:T(8,128)S(1)}, s32[2048,256]{1,0:T(8,128)}, u32[]{:S(2)}) copy-start(s32[2048,256]{1,0:T(8,128)} %get-tuple-element.21.inv_hbm) | copy-start | bytes 6291460
  74.3 22.2 %copy-start.2 = (f32[9,1024]{1,0:T(8,128)S(1)}, f32[9,1024]{1,0:T(8,128)}, u32[]{:S(2)}) copy-start(f32[9,1024]{1,0:T(8,128)} %taps_ref.1) | copy-start | bytes 110596
